TPU v7x, 32 devices: a whole 2x2x4 slice. The times are simulated.
32 devices in a mesh: groups: 2 (over x), hst: 8 (over z, y), head: 2 (over core).
Axes of the slice: x: 2, y: 2, z: 4, core: 2. Of those that a mesh axis runs over, the one named last changes fastest.
Arguments:
- ctx_query: bfloat16 [3072, 64, 128], P(('groups', 'hst'), 'head'), parts along dimension 0, may hold values from -8 to 8
- ctx_key: bfloat16 [3072, 64, 128], P(('groups', 'hst'), 'head'), parts along dimension 0, may hold values from -8 to 8
- ctx_value: bfloat16 [3072, 64, 128], P(('groups', 'hst'), 'head'), parts along dimension 0, may hold values from -6 to 6
- valid: int32 [16], P(('groups', 'hst')), parts along dimension 0, may hold values from 128 to 192
- tail_query: bfloat16 [128, 64, 128], P(('groups', 'hst'), 'head'), parts along dimension 0, may hold values from -8 to 8
- tail_position: int32 [128], P(('groups', 'hst')), parts along dimension 0, may hold values from 1 to 1536
Outputs:
- ctx_out: bfloat16 [3072, 64, 128], P(('groups', 'hst'), 'head'), parts along dimension 0
- tail_out: bfloat16 [128, 64, 128], P(('groups', 'hst'), 'head'), parts along dimension 0
There are 2 independent parts, one for each index of `groups`. A program takes and returns all parts, laid end to end along the dimension named above; each array names one. Nothing has to cross between parts.
All inputs are finite; a program needn't handle non-finite values.
Results may differ from a plain program's by a relative error of at most 0.0043.
Values may be sent and summed in bfloat16 or wider, within the bound.
No kernel may reach another device: no remote copies, remote signals or barrier semaphores. Data moves between devices by JAX's collectives and lax.ppermute only.
A program may use at most 128 MiB of HBM per device.

v0:
```python
import functools
import math

import jax
import jax.numpy as jnp
from jax import lax
from jax.experimental import pallas as pl
from jax.experimental.pallas import tpu as pltpu
from jax.sharding import PartitionSpec as P


ANCHOR = 128
GROUP = 8
NEG = -1e30
F32 = jnp.float32
BF16 = jnp.bfloat16
ANY = pl.BlockSpec(memory_space=pl.ANY)
SMEM = pl.BlockSpec(memory_space=pltpu.SMEM)


def dot(a, b, dims):
    return lax.dot_general(a, b, (dims, ((), ())), preferred_element_type=F32)


def pack_kernel(n, valid, position, query, out):
    rows, heads, width = query.shape
    row = lax.broadcasted_iota(jnp.int32, (rows, width), 0)
    lane = lax.broadcasted_iota(jnp.int32, (rows, width), 1)
    slab = jnp.where(lane == 2, valid[0], 0)
    for r in range(rows):
        high = lax.shift_right_logical(position[r], 6)
        low = jnp.bitwise_and(position[r], 63)
        slab = jnp.where((row == r) & (lane == 0), high, slab)
        slab = jnp.where((row == r) & (lane == 1), low, slab)
    slab = slab.astype(F32).astype(BF16)
    for i in range(n):
        out[i, :rows] = query[...]
        out[i, rows, :rows] = slab
        out[i, rows, rows:] = jnp.zeros((heads - rows, width), BF16)


def pack(n, valid, position, query):
    rows, heads, width = query.shape
    return pl.pallas_call(
        functools.partial(pack_kernel, n),
        out_shape=jax.ShapeDtypeStruct((n, rows + 1, heads, width), BF16),
        in_specs=[SMEM, SMEM, pl.BlockSpec(memory_space=pltpu.VMEM)],
        out_specs=pl.BlockSpec(memory_space=pltpu.VMEM),
        name="pack",
    )(valid, position, query)


def part_kernel(rows, scale, valid, query, meta, key, value, out, stats, qs, ks, vs, ms):
    step = pl.program_id(0)
    n = query.shape[0]
    block, group, width = key.shape
    total = n * rows
    me = lax.axis_index("hst")
    qs[...] = query[:, :rows].astype(F32).reshape(total * group, width)
    ks[...] = key[...].astype(F32).reshape(block * group, width)
    vs[...] = value[...].astype(F32).reshape(block * group, width)
    for i in range(n):
        ms[i * rows : (i + 1) * rows] = meta[i, 0].astype(F32)[:rows]
    info = ms[...]
    position = info[:, 0:1] * 64.0 + info[:, 1:2]
    row = lax.broadcasted_iota(jnp.int32, (total, 1), 0)
    ahead = (row < me * rows) & (lax.rem(row, rows) == 0)
    start = jnp.sum(jnp.where(ahead, info[:, 2:3], 0.0), axis=0, keepdims=True)
    slot = lax.broadcasted_iota(jnp.int32, (total, block), 1)
    place = slot.astype(F32) + start
    seen = (place < position) & (slot < valid[0])
    lane = lax.broadcasted_iota(jnp.int32, (total, width), 1)

    @pl.when(step == 0)
    def _():
        stats[...] = jnp.full((total, width), NEG, F32)

    known = stats[...]
    for h in range(group):
        q = qs[pl.ds(h, total, stride=group), :].astype(BF16)
        k = ks[pl.ds(h, block, stride=group), :].astype(BF16)
        v = vs[pl.ds(h, block, stride=group), :].astype(BF16)
        s = jnp.where(seen, dot(q, k, ((1,), (1,))) * scale, NEG)
        peak = jnp.max(s, axis=1, keepdims=True)
        w = jnp.where(seen, jnp.exp(s - peak), 0.0)
        weight = jnp.sum(w, axis=1, keepdims=True)
        w_high = w.astype(BF16)
        w_low = (w - w_high.astype(F32)).astype(BF16)
        o = dot(w_high, v, ((1,), (0,))) + dot(w_low, v, ((1,), (0,)))
        empty = weight == 0.0
        divisor = jnp.where(empty, 1.0, weight)
        o = (o / divisor).astype(BF16)
        lse = jnp.where(empty, NEG, peak + jnp.log(divisor))
        known = jnp.where(lane == step * group + h, lse, known)
        for i in range(n):
            out[i, step * group + h] = o[i * rows : (i + 1) * rows]
    stats[...] = known

    @pl.when(step == pl.num_programs(0) - 1)
    def _():
        at = pl.num_programs(0) * group
        left = stats[...]
        for piece in range(3):
            term = left.astype(BF16)
            left = left - term.astype(F32)
            for i in range(n):
                out[i, at + piece] = term[i * rows : (i + 1) * rows]


def part(valid, far, key, value, scale):
    n, rows, heads, width = far.shape
    rows -= 1
    block = key.shape[0]
    groups = heads // GROUP
    side = pl.BlockSpec((block, GROUP, width), lambda g: (0, g, 0))
    return pl.pallas_call(
        functools.partial(part_kernel, rows, scale),
        grid=(groups,),
        out_shape=jax.ShapeDtypeStruct((n, heads + 3, rows, width), BF16),
        in_specs=[
            SMEM,
            pl.BlockSpec((n, rows + 1, GROUP, width), lambda g: (0, 0, g, 0)),
            pl.BlockSpec((n, 1, GROUP, width), lambda g: (0, rows, 0, 0)),
            side,
            side,
        ],
        out_specs=pl.BlockSpec((n, heads + 3, rows, width), lambda g: (0, 0, 0, 0)),
        scratch_shapes=[
            pltpu.VMEM((n * rows, width), F32),
            pltpu.VMEM((n * rows * GROUP, width), F32),
            pltpu.VMEM((block * GROUP, width), F32),
            pltpu.VMEM((block * GROUP, width), F32),
            pltpu.VMEM((n * rows, width), F32),
        ],
        name="part",
    )(valid, far, far, key, value)


def merge_kernel(rows, heads, parts, out, shares, sums):
    n = parts.shape[0]
    lses = []
    for i in range(n):
        pieces = [parts[i, heads + p].astype(F32) for p in range(3)]
        lses.append(pieces[0] + pieces[1] + pieces[2])
    peak = functools.reduce(jnp.maximum, lses)
    weights = [jnp.exp(lse - peak) for lse in lses]
    total = functools.reduce(jnp.add, weights)
    for i in range(n):
        shares[i] = weights[i] / total
    for h in range(heads):
        acc = None
        for i in range(n):
            term = shares[i, :, h : h + 1] * parts[i, h].astype(F32)
            acc = term if acc is None else acc + term
        sums[pl.ds(h, rows, stride=heads), :] = acc
    out[...] = sums[...].reshape(out.shape).astype(BF16)


def merge(parts, rows, heads):
    n, width = parts.shape[0], parts.shape[-1]
    return pl.pallas_call(
        functools.partial(merge_kernel, rows, heads),
        out_shape=jax.ShapeDtypeStruct((rows, heads, width), BF16),
        in_specs=[pl.BlockSpec(memory_space=pltpu.VMEM)],
        out_specs=pl.BlockSpec(memory_space=pltpu.VMEM),
        scratch_shapes=[
            pltpu.VMEM((n, rows, width), F32),
            pltpu.VMEM((rows * heads, width), F32),
        ],
        name="merge",
    )(parts)


def chunk_kernel(items, key, value, *rest):
    outs, sems = rest[:-1], rest[-1]

    @pl.when(lax.axis_index("hst") == 0)
    def _():
        copies = [
            pltpu.make_async_copy(
                (key, value)[which].at[pl.ds(0, ANCHOR), pl.ds(g * GROUP, GROUP), :],
                outs[i],
                sems.at[i],
            )
            for i, (which, g) in enumerate(items)
        ]
        for copy in copies:
            copy.start()
        for copy in copies:
            copy.wait()


def chunks_of(items, key, value):
    shape = jax.ShapeDtypeStruct((ANCHOR, GROUP, key.shape[-1]), BF16)
    outs = pl.pallas_call(
        functools.partial(chunk_kernel, items),
        out_shape=[shape] * len(items),
        in_specs=[ANY, ANY],
        out_specs=[pl.BlockSpec(memory_space=pltpu.VMEM)] * len(items),
        scratch_shapes=[pltpu.SemaphoreType.DMA((len(items),))],
        name="chunks",
    )(key, value)
    return dict(zip(items, outs))


def block_kernel(first, tables, n_cand, has_prior, scale, valid, query, key, value, *rest):
    cands = rest[:n_cand]
    out = rest[n_cand + (1 if has_prior else 0)]
    qb, kb, vb, ab, ob, qs, ks, vs, aks, avs, os_, sems = rest[n_cand + (1 if has_prior else 0) + 1 :]
    block, group, width = qb.shape
    me = lax.axis_index("hst")
    heads = pl.ds(first, group)
    loads = [
        pltpu.make_async_copy(query.at[:, heads, :], qb, sems.at[0]),
        pltpu.make_async_copy(key.at[:, heads, :], kb, sems.at[1]),
        pltpu.make_async_copy(value.at[:, heads, :], vb, sems.at[2]),
    ]
    for load in loads:
        load.start()
    for which in range(2):
        own = (key, value)[which]

        @pl.when(me == 0)
        def _():
            pltpu.make_async_copy(
                own.at[pl.ds(0, ANCHOR), heads, :], ab.at[which], sems.at[3 + which]
            ).start()

        for index, devices in tables[which]:
            hit = functools.reduce(jnp.logical_or, [me == d for d in devices])

            @pl.when(hit)
            def _():
                pltpu.make_async_copy(cands[index], ab.at[which], sems.at[3 + which]).start()

    loads[0].wait()
    qs[...] = qb[...].astype(F32).reshape(block * group, width)
    loads[1].wait()
    ks[...] = kb[...].astype(F32).reshape(block * group, width)
    loads[2].wait()
    vs[...] = vb[...].astype(F32).reshape(block * group, width)
    for which, dst in ((0, aks), (1, avs)):
        pltpu.make_async_copy(
            key.at[pl.ds(0, ANCHOR), heads, :], ab.at[which], sems.at[3 + which]
        ).wait()
        dst[...] = ab[which].astype(F32).reshape(ANCHOR * group, width)

    row = lax.broadcasted_iota(jnp.int32, (block, block), 0)
    col = lax.broadcasted_iota(jnp.int32, (block, block), 1)
    seen = (col <= row) & (col < valid[0])
    anchored = jnp.where(me != 0, 0.0, NEG).astype(F32)
    for h in range(group):
        q = qs[pl.ds(h, block, stride=group), :].astype(BF16)
        k = ks[pl.ds(h, block, stride=group), :].astype(BF16)
        v = vs[pl.ds(h, block, stride=group), :].astype(BF16)
        ak = aks[pl.ds(h, ANCHOR, stride=group), :].astype(BF16)
        av = avs[pl.ds(h, ANCHOR, stride=group), :].astype(BF16)
        s = jnp.where(seen, dot(q, k, ((1,), (1,))) * scale, NEG)
        a = jnp.where(me != 0, dot(q, ak, ((1,), (1,))) * scale, NEG)
        peak = jnp.maximum(jnp.max(s, axis=1, keepdims=True), jnp.max(a, axis=1, keepdims=True))
        w = jnp.exp(s - peak)
        u = jnp.exp(a - peak)
        weight = jnp.sum(w, axis=1, keepdims=True) + jnp.sum(u, axis=1, keepdims=True)
        o = dot(w.astype(BF16), v, ((1,), (0,))) + dot(u.astype(BF16), av, ((1,), (0,)))
        os_[pl.ds(h, block, stride=group), :] = o / weight
    ob[...] = os_[...].reshape(block, group, width).astype(BF16)
    save = pltpu.make_async_copy(ob, out.at[:, heads, :], sems.at[5])
    save.start()
    save.wait()


def block_part(first, tables, cands, prior, valid, query, key, value, scale):
    block, _, width = query.shape
    operands = [valid, query, key, value, *cands]
    aliases = {}
    if prior is not None:
        aliases = {len(operands): 0}
        operands.append(prior)
    return pl.pallas_call(
        functools.partial(block_kernel, first, tables, len(cands), prior is not None, scale),
        out_shape=jax.ShapeDtypeStruct(query.shape, BF16),
        in_specs=[SMEM] + [ANY] * (len(operands) - 1),
        out_specs=ANY,
        scratch_shapes=[pltpu.VMEM((block, GROUP, width), BF16)] * 3
        + [pltpu.VMEM((2, ANCHOR, GROUP, width), BF16), pltpu.VMEM((block, GROUP, width), BF16)]
        + [pltpu.VMEM((block * GROUP, width), F32)] * 3
        + [pltpu.VMEM((ANCHOR * GROUP, width), F32)] * 2
        + [pltpu.VMEM((block * GROUP, width), F32), pltpu.SemaphoreType.DMA((6,))],
        input_output_aliases=aliases,
    )(*operands)


def schedule(n, heads):
    groups = heads // GROUP
    order = [(w, g) for g in range(groups) for w in range(2)]
    across = 2 if n % 2 == 0 else 1
    deep = n // across
    if across == 2:
        cut = len(order) // 2 + 1
        up, over = order[:cut], order[cut:]
        over = over[1:] + over[:1]
    else:
        up, over = order, []
    place = lambda z, y: z * across + y
    seq = over + up
    z_pairs, y_pairs = [], []
    found = {item: [] for item in order}
    for s in range(len(seq) + deep + 1):
        pairs = []
        for z in range(deep - 1):
            if 0 <= s - z < len(up):
                pairs.append((place(z, 0), place(z + 1, 0)))
                found[up[s - z]].append((("z", s), place(z + 1, 0)))
            if across == 2 and 0 <= s - 1 - z < len(over):
                pairs.append((place(z, 1), place(z + 1, 1)))
                found[over[s - 1 - z]].append((("z", s), place(z + 1, 1)))
        if pairs:
            z_pairs.append(pairs)
        pairs = []
        if across == 2:
            if s < len(seq):
                pairs.append((place(0, 0), place(0, 1)))
                found[seq[s]].append((("y", s), place(0, 1)))
            for z in range(1, deep):
                if 0 <= s - z < len(up):
                    pairs.append((place(z, 0), place(z, 1)))
                    found[up[s - z]].append((("y", s), place(z, 1)))
                if 0 <= s - 1 - z < len(over):
                    pairs.append((place(z, 1), place(z, 0)))
                    found[over[s - 1 - z]].append((("y", s), place(z, 0)))
        if pairs:
            y_pairs.append(pairs)
    ready = {g: max(s for w in range(2) for (_, s), _ in found[(w, g)]) for g in range(groups)}
    return up, over, z_pairs, y_pairs, found, ready


def local(n, ctx_query, ctx_key, ctx_value, valid, tail_query, tail_position):
    return body(n, ctx_query, ctx_key, ctx_value, valid, tail_query, tail_position)


def body(n, ctx_query, ctx_key, ctx_value, valid, tail_query, tail_position):
    _, heads, width = ctx_query.shape
    rows = tail_query.shape[0]
    scale = 1.0 / math.sqrt(width)
    me = lax.axis_index("hst")
    up, over, z_pairs, y_pairs, found, ready = schedule(n, heads)
    seq = over + up
    is_root, is_side = me == 0, me == 1

    first = tuple(dict.fromkeys([up[0], seq[0]]))
    chunk = chunks_of(first, ctx_key, ctx_value)
    chunk.update(chunks_of(tuple(i for i in up + over if i not in first), ctx_key, ctx_value))

    z_got, y_got = [], []
    for s in range(max(len(z_pairs), len(y_pairs))):
        z_last = z_got[s - 1] if 0 < s <= len(z_got) else None
        y_last = y_got[s - 1] if 0 < s <= len(y_got) else None
        if s < len(z_pairs):
            pay = z_last
            if pay is None:
                pay = chunk[up[s]]
            else:
                if s < len(up):
                    pay = jnp.where(is_root, chunk[up[s]], pay)
                if 1 <= s <= len(over):
                    pay = jnp.where(is_side, y_last, pay)
            z_new = lax.ppermute(pay, "hst", z_pairs[s])
        if s < len(y_pairs):
            if z_last is None:
                pay = chunk[seq[s]]
            elif s < len(seq):
                pay = jnp.where(is_root, chunk[seq[s]], z_last)
            else:
                pay = z_last
            y_got.append(lax.ppermute(pay, "hst", y_pairs[s]))
        if s < len(z_pairs):
            z_got.append(z_new)

    message = pack(n, valid, tail_position, tail_query)
    far = lax.all_to_all(message, "hst", split_axis=0, concat_axis=0, tiled=True)
    parts = part(valid, far, ctx_key, ctx_value, scale)
    back = lax.all_to_all(parts, "hst", split_axis=0, concat_axis=0, tiled=True)
    tail_out = merge(back, rows, heads)

    ctx_out = None
    for g in sorted(ready, key=ready.get):
        cands, tables = [], []
        for w in range(2):
            table = {}
            for spot, device in found[(w, g)]:
                table.setdefault(spot, []).append(device)
            entries = []
            for (axis, s), devices in table.items():
                entries.append((len(cands), devices))
                cands.append((z_got if axis == "z" else y_got)[s])
            tables.append(entries)
        ctx_out = block_part(
            g * GROUP, tables, cands, ctx_out, valid, ctx_query, ctx_key, ctx_value, scale
        )
    return (ctx_out, tail_out)


def solution(mesh):
    both = ("groups", "hst")
    wide, flat = P(both, "head", None), P(both)
    n = mesh.shape["hst"]
    return jax.shard_map(
        functools.partial(local, n),
        mesh=mesh,
        in_specs=(wide, wide, wide, flat, wide, flat),
        out_specs=(wide, wide),
        check_vma=False,
    )
```

profile of v0, /device:TPU:0, one launch (start us, length us, event | category | flops | bytes accessed | tf_op | source)
XLA Modules:
  0.0 118.2 jit_solution(14481354690693048431)
XLA Ops:
  0.6 1.9 %chunks.3 = (bf16[128,8,128]{2,1,0:T(8,128)(2,1)}, bf16[128,8,128]{2,1,0:T(8,128)(2,1)}) custom-call(bf16[192,32,128]{2,1,0:T(8,128)(2,1)} %key.13, bf16[192,32,128]{2,1,0:T(8,128)(2,1)} %value.13), custom_call_target="tpu_custom_call" | custom-call | tf_op jit(solution)/shard_map/chunks/pallas_call | solution.py:195
  2.5 3.9 %collective-permute-start.1 = (bf16[128,8,128]{2,1,0:T(8,128)(2,1)}, bf16[128,8,128]{2,1,0:T(8,128)(2,1)S(1)}, u32[]{:S(2)}, u32[]{:S(2)}) collective-permute-start(bf16[128,8,128]{2,1,0:T(8,128)(2,1)} %get-tuple-element.14), channel_id=1, source_target_pairs={{0,4},{1,5},{16,20},{17,21}} | collective-permute-start | bytes 786440 | tf_op jit(solution)/shard_map/ppermute | solution.py:367
  6.5 1.3 %collective-permute-start = (bf16[128,8,128]{2,1,0:T(8,128)(2,1)}, bf16[128,8,128]{2,1,0:T(8,128)(2,1)S(1)}, u32[]{:S(2)}, u32[]{:S(2)}) collective-permute-start(bf16[128,8,128]{2,1,0:T(8,128)(2,1)} %get-tuple-element.12), channel_id=1, source_target_pairs={{0,2},{1,3},{16,18},{17,19}} | collective-permute-start | bytes 786440 | tf_op jit(solution)/shard_map/ppermute | solution.py:375
  7.8 2.6 %chunks.2 = (bf16[128,8,128]{2,1,0:T(8,128)(2,1)}, bf16[128,8,128]{2,1,0:T(8,128)(2,1)}, bf16[128,8,128]{2,1,0:T(8,128)(2,1)}, bf16[128,8,128]{2,1,0:T(8,128)(2,...) custom-call(bf16[192,32,128]{2,1,0:T(8,128)(2,1)} %key.13, bf16[192,32,128]{2,1,0:T(8,128)(2,1)} %value.13), custom_call_target="tpu_custom_call" | custom-call | tf_op jit(solution)/shard_map/chunks/pallas_call | solution.py:195
  10.4 1.9 %collective-permute-done.1.rest_0_ = bf16[128,8,128]{2,1,0:T(8,128)(2,1)S(1)} collective-permute-done((bf16[128,8,128]{2,1,0:T(8,128)(2,1)}, bf16[128,8,128]{2,1,0:T(8,128)(2,1)S(1)}, u32[]{:S(2)}, u32[]{:S(2)}) %collective-permute-start.1) | collective-permute-done | bytes 262176 | tf_op jit(solution)/shard_map/ppermute | solution.py:367
  12.3 1.3 %collective-permute-done.rest_0_ = bf16[128,8,128]{2,1,0:T(8,128)(2,1)S(1)} collective-permute-done((bf16[128,8,128]{2,1,0:T(8,128)(2,1)}, bf16[128,8,128]{2,1,0:T(8,128)(2,1)S(1)}, u32[]{:S(2)}, u32[]{:S(2)}) %collective-permute-start) | collective-permute-done | bytes 262176 | tf_op jit(solution)/shard_map/ppermute | solution.py:375
  14.8 2.0 %collective-permute-start.2 = (bf16[128,8,128]{2,1,0:T(8,128)(2,1)S(1)}, bf16[128,8,128]{2,1,0:T(8,128)(2,1)S(1)}, u32[]{:S(2)}, u32[]{:S(2)}) collective-permute-start(bf16[128,8,128]{2,1,0:T(8,128)(2,1)S(1)} %get-tuple-element.25), channel_id=1, source_target_pairs={{0,4},{2,6},{4,8},{1,5},{3,7},{5,9},{16,20},{18,22},{20,24},{17,21... | collective-permute-start | bytes 786440 | tf_op jit(solution)/shard_map/ppermute | solution.py:367
  16.8 2.6 %collective-permute-start.4 = (bf16[128,8,128]{2,1,0:T(8,128)(2,1)S(1)}, bf16[128,8,128]{2,1,0:T(8,128)(2,1)S(1)}, u32[]{:S(2)}, u32[]{:S(2)}) collective-permute-start(bf16[128,8,128]{2,1,0:T(8,128)(2,1)S(1)} %get-tuple-element.24), channel_id=1, source_target_pairs={{0,2},{4,6},{1,3},{5,7},{16,18},{20,22},{17,19},{21,23}} | collective-permute-start | bytes 786440 | tf_op jit(solution)/shard_map/ppermute | solution.py:375
  19.4 2.1 %collective-permute-done.2.rest_1_.rest_6_ = bf16[128,8,128]{2,1,0:T(8,128)(2,1)S(1)} collective-permute-done((bf16[128,8,128]{2,1,0:T(8,128)(2,1)S(1)}, bf16[128,8,128]{2,1,0:T(8,128)(2,1)S(1)}, u32[]{:S(2)}, u32[]{:S(2)}) %collective-permute-start.2) | collective-permute-done | bytes 262176 | tf_op jit(solution)/shard_map/ppermute | solution.py:367
  21.5 2.6 %collective-permute-done.4.rest_2_.rest_7_ = bf16[128,8,128]{2,1,0:T(8,128)(2,1)S(1)} collective-permute-done((bf16[128,8,128]{2,1,0:T(8,128)(2,1)S(1)}, bf16[128,8,128]{2,1,0:T(8,128)(2,1)S(1)}, u32[]{:S(2)}, u32[]{:S(2)}) %collective-permute-start.4) | collective-permute-done | bytes 262176 | tf_op jit(solution)/shard_map/ppermute | solution.py:375
  24.2 4.4 %collective-permute-start.3 = (bf16[128,8,128]{2,1,0:T(8,128)(2,1)S(1)}, bf16[128,8,128]{2,1,0:T(8,128)(2,1)S(1)}, u32[]{:S(2)}, u32[]{:S(2)}) collective-permute-start(bf16[128,8,128]{2,1,0:T(8,128)(2,1)S(1)} %get-tuple-element.23), channel_id=1, source_target_pairs={{0,2},{4,6},{6,4},{8,10},{1,3},{5,7},{7,5},{9,11},{16,18},{20,22},... | collective-permute-start | bytes 786440 | tf_op jit(solution)/shard_map/ppermute | solution.py:375
  28.6 1.3 %collective-permute-start.5 = (bf16[128,8,128]{2,1,0:T(8,128)(2,1)S(1)}, bf16[128,8,128]{2,1,0:T(8,128)(2,1)S(1)}, u32[]{:S(2)}, u32[]{:S(2)}) collective-permute-start(bf16[128,8,128]{2,1,0:T(8,128)(2,1)S(1)} %get-tuple-element.22), channel_id=1, source_target_pairs={{0,4},{2,6},{4,8},{6,10},{8,12},{1,5},{3,7},{5,9},{7,11},{9,13},{1... | collective-permute-start | bytes 786440 | tf_op jit(solution)/shard_map/ppermute | solution.py:367
  29.9 2.5 %collective-permute-done.3.rest_4_.rest_8_.rest_3_.rest_6_ = bf16[128,8,128]{2,1,0:T(8,128)(2,1)S(1)} collective-permute-done((bf16[128,8,128]{2,1,0:T(8,128)(2,1)S(1)}, bf16[128,8,128]{2,1,0:T(8,128)(2,1)S(1)}, u32[]{:S(2)}, u32[]{:S(2)}) %collective-permute-start.3) | collective-permute-done | bytes 262176 | tf_op jit(solution)/shard_map/ppermute | solution.py:375
  32.5 1.3 %collective-permute-done.5.rest_3_.rest_7_.rest_2_.rest_8_.rest_0_ = bf16[128,8,128]{2,1,0:T(8,128)(2,1)S(1)} collective-permute-done((bf16[128,8,128]{2,1,0:T(8,128)(2,1)S(1)}, bf16[128,8,128]{2,1,0:T(8,128)(2,1)S(1)}, u32[]{:S(2)}, u32[]{:S(2)}) %collective-permute-start.5) | collective-permute-done | bytes 262176 | tf_op jit(solution)/shard_map/ppermute | solution.py:367
  33.9 4.5 %collective-permute-start.6 = (bf16[128,8,128]{2,1,0:T(8,128)(2,1)S(1)}, bf16[128,8,128]{2,1,0:T(8,128)(2,1)S(1)}, u32[]{:S(2)}, u32[]{:S(2)}) collective-permute-start(bf16[128,8,128]{2,1,0:T(8,128)(2,1)S(1)} %get-tuple-element.19), channel_id=1, source_target_pairs={{0,4},{2,6},{4,8},{6,10},{8,12},{10,14},{1,5},{3,7},{5,9},{7,11},{... | collective-permute-start | bytes 786440 | tf_op jit(solution)/shard_map/ppermute | solution.py:367
  39.1 1.7 %pack.1 = bf16[8,9,32,128]{3,2,1,0:T(8,128)(2,1)} custom-call(s32[1]{0:T(128)S(6)} %copy.14.valid, s32[8]{0:T(128)} %position.1, bf16[8,32,128]{2,1,0:T(8,128)(2,1)} %query.9), custom_call_target="tpu_custom_call" | custom-call | tf_op jit(solution)/shard_map/pack/pallas_call | solution.py:44
  40.8 3.5 %all-to-all-start = ((bf16[8,9,32,128]{3,2,1,0:T(8,128)(2,1)}), bf16[8,9,32,128]{3,2,1,0:T(8,128)(2,1)S(1)}, u32[]{:S(2)}, u32[]{:S(2)}) async-start(bf16[8,9,32,128]{3,2,1,0:T(8,128)(2,1)} %pack.1), calls=%async_computation | async-start | bytes 1179648 | tf_op jit(solution)/shard_map/all_to_all | solution.py:380
  44.5 3.8 %collective-permute-start.7 = (bf16[128,8,128]{2,1,0:T(8,128)(2,1)S(1)}, bf16[128,8,128]{2,1,0:T(8,128)(2,1)S(1)}, u32[]{:S(2)}, u32[]{:S(2)}) collective-permute-start(bf16[128,8,128]{2,1,0:T(8,128)(2,1)S(1)} %get-tuple-element.21), channel_id=1, source_target_pairs={{0,4},{4,8},{6,10},{8,12},{10,14},{1,5},{5,9},{7,11},{9,13},{11,15... | collective-permute-start | bytes 786440 | tf_op jit(solution)/shard_map/ppermute | solution.py:367
  48.3 9.1 %collective-permute-done.7.rest_11_.rest_3_.rest_7_.rest_0_.rest_8_ = bf16[128,8,128]{2,1,0:T(8,128)(2,1)S(1)} collective-permute-done((bf16[128,8,128]{2,1,0:T(8,128)(2,1)S(1)}, bf16[128,8,128]{2,1,0:T(8,128)(2,1)S(1)}, u32[]{:S(2)}, u32[]{:S(2)}) %collective-permute-start.7) | collective-permute-done | bytes 262176 | tf_op jit(solution)/shard_map/ppermute | solution.py:367
  58.9 6.6 %part.1 = bf16[8,35,8,128]{3,2,1,0:T(8,128)(2,1)} custom-call(s32[1]{0:T(128)S(6)} %copy.14.valid, bf16[8,9,32,128]{3,2,1,0:T(8,128)(2,1)} %copy-done.7, bf16[8,9,32,128]{3,2,1,0:T(8,128)(2,1)} %copy-done.7, bf16[192,32,128]{2,1,0:T(8,128)(2,1)} %key.13, bf16[192,32,128]{2,1,0:T(8,128)(2,1)} %value.13), custom_call_target="tpu_custom_call" | custom-call | tf_op jit(solution)/shard_map/part/pallas_call | solution.py:116
  65.5 9.0 %all-to-all-start.1 = ((bf16[8,35,8,128]{3,2,1,0:T(8,128)(2,1)}), bf16[8,35,8,128]{3,2,1,0:T(8,128)(2,1)S(1)}, u32[]{:S(2)}, u32[]{:S(2)}) async-start(bf16[8,35,8,128]{3,2,1,0:T(8,128)(2,1)} %part.1), calls=%async_computation.1 | async-start | bytes 1146880 | tf_op jit(solution)/shard_map/all_to_all | solution.py:382
  74.6 3.9 %collective-permute-start.14 = (bf16[128,8,128]{2,1,0:T(8,128)(2,1)S(1)}, bf16[128,8,128]{2,1,0:T(8,128)(2,1)S(1)}, u32[]{:S(2)}, u32[]{:S(2)}) collective-permute-start(bf16[128,8,128]{2,1,0:T(8,128)(2,1)S(1)} %get-tuple-element.18), channel_id=1, source_target_pairs={{0,2},{4,6},{6,4},{8,10},{10,8},{12,14},{1,3},{5,7},{7,5},{9,11},{... | collective-permute-start | bytes 786440 | tf_op jit(solution)/shard_map/ppermute | solution.py:375
  78.5 1.3 %collective-permute-start.13 = (bf16[128,8,128]{2,1,0:T(8,128)(2,1)S(1)}, bf16[128,8,128]{2,1,0:T(8,128)(2,1)S(1)}, u32[]{:S(2)}, u32[]{:S(2)}) collective-permute-start(bf16[128,8,128]{2,1,0:T(8,128)(2,1)S(1)} %get-tuple-element.20), channel_id=1, source_target_pairs={{0,2},{4,6},{6,4},{8,10},{10,8},{12,14},{14,12},{1,3},{5,7},{7,5},... | collective-permute-start | bytes 786440 | tf_op jit(solution)/shard_map/ppermute | solution.py:375
  81.3 1.3 %collective-permute-start.9 = (bf16[128,8,128]{2,1,0:T(8,128)(2,1)}, bf16[128,8,128]{2,1,0:T(8,128)(2,1)S(1)}, u32[]{:S(2)}, u32[]{:S(2)}) collective-permute-start(bf16[128,8,128]{2,1,0:T(8,128)(2,1)} %broadcast_select_fusion.4), channel_id=1, source_target_pairs={{0,2},{4,6},{8,10},{10,8},{12,14},{14,12},{1,3},{5,7},{9,11},{11,9... | collective-permute-start | bytes 786440 | tf_op jit(solution)/shard_map/ppermute | solution.py:375
  82.6 1.3 %collective-permute-start.11 = (bf16[128,8,128]{2,1,0:T(8,128)(2,1)S(1)}, bf16[128,8,128]{2,1,0:T(8,128)(2,1)S(1)}, u32[]{:S(2)}, u32[]{:S(2)}) collective-permute-start(bf16[128,8,128]{2,1,0:T(8,128)(2,1)S(1)} %broadcast_select_fusion.3), channel_id=1, source_target_pairs={{0,2},{8,10},{12,14},{14,12},{1,3},{9,11},{13,15},{15,13},{16,18},... | collective-permute-start | bytes 786440 | tf_op jit(solution)/shard_map/ppermute | solution.py:375
  84.0 1.5 %collective-permute-start.12 = (bf16[128,8,128]{2,1,0:T(8,128)(2,1)S(1)}, bf16[128,8,128]{2,1,0:T(8,128)(2,1)S(1)}, u32[]{:S(2)}, u32[]{:S(2)}) collective-permute-start(bf16[128,8,128]{2,1,0:T(8,128)(2,1)S(1)} %broadcast_select_fusion.2), channel_id=1, source_target_pairs={{0,2},{12,14},{1,3},{13,15},{16,18},{28,30},{17,19},{29,31}} | collective-permute-start | bytes 786440 | tf_op jit(solution)/shard_map/ppermute | solution.py:375
  86.4 6.5 %collective-permute-done.13.rest_11_.rest_6_.rest_12_.rest_4_.rest_8_.rest_9_ = bf16[128,8,128]{2,1,0:T(8,128)(2,1)S(1)} collective-permute-done((bf16[128,8,128]{2,1,0:T(8,128)(2,1)S(1)}, bf16[128,8,128]{2,1,0:T(8,128)(2,1)S(1)}, u32[]{:S(2)}, u32[]{:S(2)}) %collective-permute-start.13) | collective-permute-done | bytes 262176 | tf_op jit(solution)/shard_map/ppermute | solution.py:375
  93.6 4.7 %shard_map.77.rest_14_ = bf16[192,32,128]{2,1,0:T(8,128)(2,1)} custom-call(s32[1]{0:T(128)S(6)} %copy.14.valid, bf16[192,32,128]{2,1,0:T(8,128)(2,1)} %query.8, bf16[192,32,128]{2,1,0:T(8,128)(2,1)} %key.13, bf16[192,32,128]{2,1,0:T(8,128)(2,1)} %value.13, bf16[128,8,128]{2,1,0:T(8,128)(2,1)} %copy-done.14, bf16[128,8,128]{2,1,0:T(8,128)(2,1)} %copy-done.8, ...), custom_call_target="tpu_custom_call" | custom-call | tf_op jit(solution)/shard_map/pallas_call | solution.py:279
  99.3 4.8 %shard_map.78.rest_12_ = bf16[192,32,128]{2,1,0:T(8,128)(2,1)} custom-call(s32[1]{0:T(128)S(6)} %copy.14.valid, bf16[192,32,128]{2,1,0:T(8,128)(2,1)} %query.8, bf16[192,32,128]{2,1,0:T(8,128)(2,1)} %key.13, bf16[192,32,128]{2,1,0:T(8,128)(2,1)} %value.13, bf16[128,8,128]{2,1,0:T(8,128)(2,1)} %copy-done.13, ...), custom_call_target="tpu_custom_call", output_to_operand_aliasing={{}: (18, {})} | custom-call | tf_op jit(solution)/shard_map/pallas_call | solution.py:279
  104.8 4.7 %shard_map.79.rest_13_ = bf16[192,32,128]{2,1,0:T(8,128)(2,1)} custom-call(s32[1]{0:T(128)S(6)} %copy.14.valid, bf16[192,32,128]{2,1,0:T(8,128)(2,1)} %query.8, bf16[192,32,128]{2,1,0:T(8,128)(2,1)} %key.13, bf16[192,32,128]{2,1,0:T(8,128)(2,1)} %value.13, bf16[128,8,128]{2,1,0:T(8,128)(2,1)} %copy-done.2, ...), custom_call_target="tpu_custom_call", output_to_operand_aliasing={{}: (16, {})} | custom-call | tf_op jit(solution)/shard_map/pallas_call | solution.py:279
  110.4 2.1 %merge.1 = bf16[8,32,128]{2,1,0:T(8,128)(2,1)} custom-call(bf16[8,35,8,128]{3,2,1,0:T(8,128)(2,1)} %copy-done.12), custom_call_target="tpu_custom_call" | custom-call | tf_op jit(solution)/shard_map/merge/pallas_call | solution.py:161
  113.3 4.8 %shard_map.80 = bf16[192,32,128]{2,1,0:T(8,128)(2,1)} custom-call(s32[1]{0:T(128)S(6)} %copy.14.valid, bf16[192,32,128]{2,1,0:T(8,128)(2,1)} %query.8, bf16[192,32,128]{2,1,0:T(8,128)(2,1)} %key.13, bf16[192,32,128]{2,1,0:T(8,128)(2,1)} %value.13, bf16[128,8,128]{2,1,0:T(8,128)(2,1)} %copy-done.3, ...), custom_call_target="tpu_custom_call", output_to_operand_aliasing={{}: (17, {})} | custom-call | tf_op jit(solution)/shard_map/pallas_call | solution.py:279
  (64 shorter events, 9.2 us)
Async XLA Ops:
  2.5 9.8 %collective-permute-start.1 = (bf16[128,8,128]{2,1,0:T(8,128)(2,1)}, bf16[128,8,128]{2,1,0:T(8,128)(2,1)S(1)}, u32[]{:S(2)}, u32[]{:S(2)}) collective-permute-start(bf16[128,8,128]{2,1,0:T(8,128)(2,1)} %get-tuple-element.14), channel_id=1, source_target_pairs={{0,4},{1,5},{16,20},{17,21}} | collective-permute-start | bytes 786440 | tf_op jit(solution)/shard_map/ppermute | solution.py:367
  6.5 7.2 %collective-permute-start = (bf16[128,8,128]{2,1,0:T(8,128)(2,1)}, bf16[128,8,128]{2,1,0:T(8,128)(2,1)S(1)}, u32[]{:S(2)}, u32[]{:S(2)}) collective-permute-start(bf16[128,8,128]{2,1,0:T(8,128)(2,1)} %get-tuple-element.12), channel_id=1, source_target_pairs={{0,2},{1,3},{16,18},{17,19}} | collective-permute-start | bytes 786440 | tf_op jit(solution)/shard_map/ppermute | solution.py:375
  10.4 13.7 %copy-start.19 = (bf16[128,8,128]{2,1,0:T(8,128)(2,1)S(1)}, bf16[128,8,128]{2,1,0:T(8,128)(2,1)}, u32[]{:S(2)}) copy-start(bf16[128,8,128]{2,1,0:T(8,128)(2,1)} %get-tuple-element.17) | copy-start | bytes 786436
  10.4 13.7 %copy-start.22 = (bf16[128,8,128]{2,1,0:T(8,128)(2,1)S(1)}, bf16[128,8,128]{2,1,0:T(8,128)(2,1)}, u32[]{:S(2)}) copy-start(bf16[128,8,128]{2,1,0:T(8,128)(2,1)} %get-tuple-element.11) | copy-start | bytes 786436
  12.3 11.9 %copy-start.14 = (bf16[128,8,128]{2,1,0:T(8,128)(2,1)}, bf16[128,8,128]{2,1,0:T(8,128)(2,1)S(1)}, u32[]{:S(2)}) copy-start(bf16[128,8,128]{2,1,0:T(8,128)(2,1)S(1)} %collective-permute-done.1.rest_0_) | copy-start | bytes 786436
  13.6 10.6 %copy-start.13 = (bf16[128,8,128]{2,1,0:T(8,128)(2,1)}, bf16[128,8,128]{2,1,0:T(8,128)(2,1)S(1)}, u32[]{:S(2)}) copy-start(bf16[128,8,128]{2,1,0:T(8,128)(2,1)S(1)} %collective-permute-done.rest_0_) | copy-start | bytes 786436
  13.6 20.2 %copy-start.18 = (bf16[128,8,128]{2,1,0:T(8,128)(2,1)S(1)}, bf16[128,8,128]{2,1,0:T(8,128)(2,1)}, u32[]{:S(2)}) copy-start(bf16[128,8,128]{2,1,0:T(8,128)(2,1)} %get-tuple-element.15) | copy-start | bytes 786436
  13.6 20.2 %copy-start.21 = (bf16[128,8,128]{2,1,0:T(8,128)(2,1)S(1)}, bf16[128,8,128]{2,1,0:T(8,128)(2,1)}, u32[]{:S(2)}) copy-start(bf16[128,8,128]{2,1,0:T(8,128)(2,1)} %get-tuple-element.14) | copy-start | bytes 786436
  14.8 6.7 %collective-permute-start.2 = (bf16[128,8,128]{2,1,0:T(8,128)(2,1)S(1)}, bf16[128,8,128]{2,1,0:T(8,128)(2,1)S(1)}, u32[]{:S(2)}, u32[]{:S(2)}) collective-permute-start(bf16[128,8,128]{2,1,0:T(8,128)(2,1)S(1)} %get-tuple-element.25), channel_id=1, source_target_pairs={{0,4},{2,6},{4,8},{1,5},{3,7},{5,9},{16,20},{18,22},{20,24},{17,21... | collective-permute-start | bytes 786440 | tf_op jit(solution)/shard_map/ppermute | solution.py:367
  16.8 7.3 %collective-permute-start.4 = (bf16[128,8,128]{2,1,0:T(8,128)(2,1)S(1)}, bf16[128,8,128]{2,1,0:T(8,128)(2,1)S(1)}, u32[]{:S(2)}, u32[]{:S(2)}) collective-permute-start(bf16[128,8,128]{2,1,0:T(8,128)(2,1)S(1)} %get-tuple-element.24), channel_id=1, source_target_pairs={{0,2},{4,6},{1,3},{5,7},{16,18},{20,22},{17,19},{21,23}} | collective-permute-start | bytes 786440 | tf_op jit(solution)/shard_map/ppermute | solution.py:375
  21.5 12.4 %copy-start.8 = (bf16[128,8,128]{2,1,0:T(8,128)(2,1)}, bf16[128,8,128]{2,1,0:T(8,128)(2,1)S(1)}, u32[]{:S(2)}) copy-start(bf16[128,8,128]{2,1,0:T(8,128)(2,1)S(1)} %collective-permute-done.2.rest_1_.rest_6_) | copy-start | bytes 786436
  24.1 9.8 %copy-start.11 = (bf16[128,8,128]{2,1,0:T(8,128)(2,1)}, bf16[128,8,128]{2,1,0:T(8,128)(2,1)S(1)}, u32[]{:S(2)}) copy-start(bf16[128,8,128]{2,1,0:T(8,128)(2,1)S(1)} %collective-permute-done.4.rest_2_.rest_7_) | copy-start | bytes 786436
  24.2 8.3 %collective-permute-start.3 = (bf16[128,8,128]{2,1,0:T(8,128)(2,1)S(1)}, bf16[128,8,128]{2,1,0:T(8,128)(2,1)S(1)}, u32[]{:S(2)}, u32[]{:S(2)}) collective-permute-start(bf16[128,8,128]{2,1,0:T(8,128)(2,1)S(1)} %get-tuple-element.23), channel_id=1, source_target_pairs={{0,2},{4,6},{6,4},{8,10},{1,3},{5,7},{7,5},{9,11},{16,18},{20,22},... | collective-permute-start | bytes 786440 | tf_op jit(solution)/shard_map/ppermute | solution.py:375
  28.6 5.2 %collective-permute-start.5 = (bf16[128,8,128]{2,1,0:T(8,128)(2,1)S(1)}, bf16[128,8,128]{2,1,0:T(8,128)(2,1)S(1)}, u32[]{:S(2)}, u32[]{:S(2)}) collective-permute-start(bf16[128,8,128]{2,1,0:T(8,128)(2,1)S(1)} %get-tuple-element.22), channel_id=1, source_target_pairs={{0,4},{2,6},{4,8},{6,10},{8,12},{1,5},{3,7},{5,9},{7,11},{9,13},{1... | collective-permute-start | bytes 786440 | tf_op jit(solution)/shard_map/ppermute | solution.py:367
  32.5 8.4 %copy-start.6 = (bf16[128,8,128]{2,1,0:T(8,128)(2,1)}, bf16[128,8,128]{2,1,0:T(8,128)(2,1)S(1)}, u32[]{:S(2)}) copy-start(bf16[128,8,128]{2,1,0:T(8,128)(2,1)S(1)} %collective-permute-done.3.rest_4_.rest_8_.rest_3_.rest_6_) | copy-start | bytes 786436
  33.8 10.6 %copy-start.15 = (bf16[128,8,128]{2,1,0:T(8,128)(2,1)S(1)}, bf16[128,8,128]{2,1,0:T(8,128)(2,1)}, u32[]{:S(2)}) copy-start(bf16[128,8,128]{2,1,0:T(8,128)(2,1)} %get-tuple-element.10) | copy-start | bytes 786436
  33.8 10.6 %copy-start.16 = (bf16[128,8,128]{2,1,0:T(8,128)(2,1)S(1)}, bf16[128,8,128]{2,1,0:T(8,128)(2,1)}, u32[]{:S(2)}) copy-start(bf16[128,8,128]{2,1,0:T(8,128)(2,1)} %get-tuple-element.13) | copy-start | bytes 786436
  33.9 10.5 %collective-permute-start.6 = (bf16[128,8,128]{2,1,0:T(8,128)(2,1)S(1)}, bf16[128,8,128]{2,1,0:T(8,128)(2,1)S(1)}, u32[]{:S(2)}, u32[]{:S(2)}) collective-permute-start(bf16[128,8,128]{2,1,0:T(8,128)(2,1)S(1)} %get-tuple-element.19), channel_id=1, source_target_pairs={{0,4},{2,6},{4,8},{6,10},{8,12},{10,14},{1,5},{3,7},{5,9},{7,11},{... | collective-permute-start | bytes 786440 | tf_op jit(solution)/shard_map/ppermute | solution.py:367
  40.8 17.3 %all-to-all-start = ((bf16[8,9,32,128]{3,2,1,0:T(8,128)(2,1)}), bf16[8,9,32,128]{3,2,1,0:T(8,128)(2,1)S(1)}, u32[]{:S(2)}, u32[]{:S(2)}) async-start(bf16[8,9,32,128]{3,2,1,0:T(8,128)(2,1)} %pack.1), calls=%async_computation | async-start | bytes 1179648 | tf_op jit(solution)/shard_map/all_to_all | solution.py:380
  44.4 21.2 %copy-start = (bf16[128,8,128]{2,1,0:T(8,128)(2,1)}, bf16[128,8,128]{2,1,0:T(8,128)(2,1)S(1)}, u32[]{:S(2)}) copy-start(bf16[128,8,128]{2,1,0:T(8,128)(2,1)S(1)} %collective-permute-done.6.rest_9_.rest_4_.rest_1_.rest_6_.rest_7_) | copy-start | bytes 786436
  44.5 13.0 %collective-permute-start.7 = (bf16[128,8,128]{2,1,0:T(8,128)(2,1)S(1)}, bf16[128,8,128]{2,1,0:T(8,128)(2,1)S(1)}, u32[]{:S(2)}, u32[]{:S(2)}) collective-permute-start(bf16[128,8,128]{2,1,0:T(8,128)(2,1)S(1)} %get-tuple-element.21), channel_id=1, source_target_pairs={{0,4},{4,8},{6,10},{8,12},{10,14},{1,5},{5,9},{7,11},{9,13},{11,15... | collective-permute-start | bytes 786440 | tf_op jit(solution)/shard_map/ppermute | solution.py:367
  57.4 23.1 %copy-start.3 = (bf16[128,8,128]{2,1,0:T(8,128)(2,1)}, bf16[128,8,128]{2,1,0:T(8,128)(2,1)S(1)}, u32[]{:S(2)}) copy-start(bf16[128,8,128]{2,1,0:T(8,128)(2,1)S(1)} %collective-permute-done.7.rest_11_.rest_3_.rest_7_.rest_0_.rest_8_) | copy-start | bytes 786436
  57.4 22.4 %collective-permute-start.8 = (bf16[128,8,128]{2,1,0:T(8,128)(2,1)S(1)}, bf16[128,8,128]{2,1,0:T(8,128)(2,1)S(1)}, u32[]{:S(2)}, u32[]{:S(2)}) collective-permute-start(bf16[128,8,128]{2,1,0:T(8,128)(2,1)S(1)} %collective-permute-done.7.rest_11_.rest_3_.rest_7_.rest_0_.rest_8_), channel_id=1, source_target_pairs={{4,8},{8,12},{10,14},{5,9},{9,13},{11,15},{20,24},{24,28},{26,30},... | collective-permute-start | bytes 786440 | tf_op jit(solution)/shard_map/ppermute | solution.py:367
  65.5 44.1 %all-to-all-start.1 = ((bf16[8,35,8,128]{3,2,1,0:T(8,128)(2,1)}), bf16[8,35,8,128]{3,2,1,0:T(8,128)(2,1)S(1)}, u32[]{:S(2)}, u32[]{:S(2)}) async-start(bf16[8,35,8,128]{3,2,1,0:T(8,128)(2,1)} %part.1), calls=%async_computation.1 | async-start | bytes 1146880 | tf_op jit(solution)/shard_map/all_to_all | solution.py:382
  74.6 11.8 %collective-permute-start.14 = (bf16[128,8,128]{2,1,0:T(8,128)(2,1)S(1)}, bf16[128,8,128]{2,1,0:T(8,128)(2,1)S(1)}, u32[]{:S(2)}, u32[]{:S(2)}) collective-permute-start(bf16[128,8,128]{2,1,0:T(8,128)(2,1)S(1)} %get-tuple-element.18), channel_id=1, source_target_pairs={{0,2},{4,6},{6,4},{8,10},{10,8},{12,14},{1,3},{5,7},{7,5},{9,11},{... | collective-permute-start | bytes 786440 | tf_op jit(solution)/shard_map/ppermute | solution.py:375
  78.5 14.4 %collective-permute-start.13 = (bf16[128,8,128]{2,1,0:T(8,128)(2,1)S(1)}, bf16[128,8,128]{2,1,0:T(8,128)(2,1)S(1)}, u32[]{:S(2)}, u32[]{:S(2)}) collective-permute-start(bf16[128,8,128]{2,1,0:T(8,128)(2,1)S(1)} %get-tuple-element.20), channel_id=1, source_target_pairs={{0,2},{4,6},{6,4},{8,10},{10,8},{12,14},{14,12},{1,3},{5,7},{7,5},... | collective-permute-start | bytes 786440 | tf_op jit(solution)/shard_map/ppermute | solution.py:375
  79.8 18.5 %copy-start.9 = (bf16[128,8,128]{2,1,0:T(8,128)(2,1)}, bf16[128,8,128]{2,1,0:T(8,128)(2,1)S(1)}, u32[]{:S(2)}) copy-start(bf16[128,8,128]{2,1,0:T(8,128)(2,1)S(1)} %collective-permute-done.8.rest_9_.rest_1_.rest_10_) | copy-start | bytes 786436
  79.8 4.1 %collective-permute-start.10 = (bf16[128,8,128]{2,1,0:T(8,128)(2,1)S(1)}, bf16[128,8,128]{2,1,0:T(8,128)(2,1)S(1)}, u32[]{:S(2)}, u32[]{:S(2)}) collective-permute-start(bf16[128,8,128]{2,1,0:T(8,128)(2,1)S(1)} %collective-permute-done.8.rest_9_.rest_1_.rest_10_), channel_id=1, source_target_pairs={{8,12},{9,13},{24,28},{25,29}} | collective-permute-start | bytes 786440 | tf_op jit(solution)/shard_map/ppermute | solution.py:367
  81.3 17.3 %collective-permute-start.9 = (bf16[128,8,128]{2,1,0:T(8,128)(2,1)}, bf16[128,8,128]{2,1,0:T(8,128)(2,1)S(1)}, u32[]{:S(2)}, u32[]{:S(2)}) collective-permute-start(bf16[128,8,128]{2,1,0:T(8,128)(2,1)} %broadcast_select_fusion.4), channel_id=1, source_target_pairs={{0,2},{4,6},{8,10},{10,8},{12,14},{14,12},{1,3},{5,7},{9,11},{11,9... | collective-permute-start | bytes 786440 | tf_op jit(solution)/shard_map/ppermute | solution.py:375
  82.6 21.5 %collective-permute-start.11 = (bf16[128,8,128]{2,1,0:T(8,128)(2,1)S(1)}, bf16[128,8,128]{2,1,0:T(8,128)(2,1)S(1)}, u32[]{:S(2)}, u32[]{:S(2)}) collective-permute-start(bf16[128,8,128]{2,1,0:T(8,128)(2,1)S(1)} %broadcast_select_fusion.3), channel_id=1, source_target_pairs={{0,2},{8,10},{12,14},{14,12},{1,3},{9,11},{13,15},{15,13},{16,18},... | collective-permute-start | bytes 786440 | tf_op jit(solution)/shard_map/ppermute | solution.py:375
  83.9 14.4 %copy-start.17 = (bf16[128,8,128]{2,1,0:T(8,128)(2,1)}, bf16[128,8,128]{2,1,0:T(8,128)(2,1)S(1)}, u32[]{:S(2)}) copy-start(bf16[128,8,128]{2,1,0:T(8,128)(2,1)S(1)} %collective-permute-done.10.rest_3_) | copy-start | bytes 786436
  84.0 28.6 %collective-permute-start.12 = (bf16[128,8,128]{2,1,0:T(8,128)(2,1)S(1)}, bf16[128,8,128]{2,1,0:T(8,128)(2,1)S(1)}, u32[]{:S(2)}, u32[]{:S(2)}) collective-permute-start(bf16[128,8,128]{2,1,0:T(8,128)(2,1)S(1)} %broadcast_select_fusion.2), channel_id=1, source_target_pairs={{0,2},{12,14},{1,3},{13,15},{16,18},{28,30},{17,19},{29,31}} | collective-permute-start | bytes 786440 | tf_op jit(solution)/shard_map/ppermute | solution.py:375
  (8 other events, 18.0 us)
where the time goes:
time: 119 us; the launch traced here: 118 us
  starting transfers between devices  47.1 us (40%)
  Pallas kernels  34 us (29%)
  waiting for transfers between devices  28.5 us (24%)
  local copies, waits for them, and re-layouts  4.51 us (4%)
  other arithmetic  2.16 us (2%)
  between operations  1.86 us (2%)
    pallas_call x4, Pallas kernels, block_part(): pl.pallas_call(functools.partial(block_kernel, first, tables, len(cands),...  19.1 us
    ppermute x8, starting transfers between devices, body(): y_got.append(lax.ppermute(pay, 'hst', y_pairs[s]))  17.6 us
    ppermute x7, starting transfers between devices, body(): z_new = lax.ppermute(pay, 'hst', z_pairs[s])  17 us
    ppermute x7, waiting for transfers between devices, body(): z_new = lax.ppermute(pay, 'hst', z_pairs[s])  14.4 us
    ppermute x8, waiting for transfers between devices, body(): y_got.append(lax.ppermute(pay, 'hst', y_pairs[s]))  14.1 us
    all_to_all x1, starting transfers between devices, body(): back = lax.all_to_all(parts, 'hst', split_axis=0, concat_axis=0, tiled=True)  9.02 us
    pallas_call x1, Pallas kernels, part(): pl.pallas_call(functools.partial(part_kernel, rows, scale), grid=(groups,...  6.6 us
    unnamed x46, local copies, waits for them, and re-layouts  4.51 us
  transfers between devices with their start and end apart: 17, of which 10 were waited for; matrix products, arithmetic and copies ran while one was open for 1% of the time, Pallas kernels for 23%

commit v1 on v0

--- a/solution.py
+++ b/solution.py
@@ -11,6 +11,7 @@
 
 ANCHOR = 128
 GROUP = 8
+PAIR = 4
 NEG = -1e30
 F32 = jnp.float32
 BF16 = jnp.bfloat16
@@ -76,24 +77,26 @@
         stats[...] = jnp.full((total, width), NEG, F32)
 
     known = stats[...]
-    for h in range(group):
-        q = qs[pl.ds(h, total, stride=group), :].astype(BF16)
-        k = ks[pl.ds(h, block, stride=group), :].astype(BF16)
-        v = vs[pl.ds(h, block, stride=group), :].astype(BF16)
-        s = jnp.where(seen, dot(q, k, ((1,), (1,))) * scale, NEG)
-        peak = jnp.max(s, axis=1, keepdims=True)
-        w = jnp.where(seen, jnp.exp(s - peak), 0.0)
-        weight = jnp.sum(w, axis=1, keepdims=True)
-        w_high = w.astype(BF16)
-        w_low = (w - w_high.astype(F32)).astype(BF16)
-        o = dot(w_high, v, ((1,), (0,))) + dot(w_low, v, ((1,), (0,)))
-        empty = weight == 0.0
-        divisor = jnp.where(empty, 1.0, weight)
-        o = (o / divisor).astype(BF16)
-        lse = jnp.where(empty, NEG, peak + jnp.log(divisor))
+    each = range(group)
+    q = [qs[pl.ds(h, total, stride=group), :].astype(BF16) for h in each]
+    k = [ks[pl.ds(h, block, stride=group), :].astype(BF16) for h in each]
+    v = [vs[pl.ds(h, block, stride=group), :].astype(BF16) for h in each]
+    s = [jnp.where(seen, dot(q[h], k[h], ((1,), (1,))) * scale, NEG) for h in each]
+    peak = [jnp.max(s[h], axis=1, keepdims=True) for h in each]
+    w = [jnp.where(seen, jnp.exp(s[h] - peak[h]), 0.0) for h in each]
+    weight = [jnp.sum(w[h], axis=1, keepdims=True) for h in each]
+    high = [w[h].astype(BF16) for h in each]
+    low = [(w[h] - high[h].astype(F32)).astype(BF16) for h in each]
+    o = [dot(high[h], v[h], ((1,), (0,))) + dot(low[h], v[h], ((1,), (0,))) for h in each]
+    for h in each:
+        empty = weight[h] == 0.0
+        divisor = jnp.where(empty, 1.0, weight[h])
+        lse = jnp.where(empty, NEG, peak[h] + jnp.log(divisor))
         known = jnp.where(lane == step * group + h, lse, known)
+        o[h] = (o[h] / divisor).astype(BF16)
+    for h in each:
         for i in range(n):
-            out[i, step * group + h] = o[i * rows : (i + 1) * rows]
+            out[i, step * group + h] = o[h][i * rows : (i + 1) * rows]
     stats[...] = known
 
     @pl.when(step == pl.num_programs(0) - 1)
@@ -249,20 +252,27 @@
     col = lax.broadcasted_iota(jnp.int32, (block, block), 1)
     seen = (col <= row) & (col < valid[0])
     anchored = jnp.where(me != 0, 0.0, NEG).astype(F32)
-    for h in range(group):
-        q = qs[pl.ds(h, block, stride=group), :].astype(BF16)
-        k = ks[pl.ds(h, block, stride=group), :].astype(BF16)
-        v = vs[pl.ds(h, block, stride=group), :].astype(BF16)
-        ak = aks[pl.ds(h, ANCHOR, stride=group), :].astype(BF16)
-        av = avs[pl.ds(h, ANCHOR, stride=group), :].astype(BF16)
-        s = jnp.where(seen, dot(q, k, ((1,), (1,))) * scale, NEG)
-        a = jnp.where(me != 0, dot(q, ak, ((1,), (1,))) * scale, NEG)
-        peak = jnp.maximum(jnp.max(s, axis=1, keepdims=True), jnp.max(a, axis=1, keepdims=True))
-        w = jnp.exp(s - peak)
-        u = jnp.exp(a - peak)
-        weight = jnp.sum(w, axis=1, keepdims=True) + jnp.sum(u, axis=1, keepdims=True)
-        o = dot(w.astype(BF16), v, ((1,), (0,))) + dot(u.astype(BF16), av, ((1,), (0,)))
-        os_[pl.ds(h, block, stride=group), :] = o / weight
+    for base in range(0, group, PAIR):
+        each = range(base, base + PAIR)
+        take = lambda ref, size: [ref[pl.ds(h, size, stride=group), :].astype(BF16) for h in each]
+        q, k, v = take(qs, block), take(ks, block), take(vs, block)
+        ak, av = take(aks, ANCHOR), take(avs, ANCHOR)
+        each = range(PAIR)
+        s = [jnp.where(seen, dot(q[h], k[h], ((1,), (1,))) * scale, NEG) for h in each]
+        a = [jnp.where(me != 0, dot(q[h], ak[h], ((1,), (1,))) * scale, NEG) for h in each]
+        peak = [
+            jnp.maximum(jnp.max(s[h], 1, keepdims=True), jnp.max(a[h], 1, keepdims=True))
+            for h in each
+        ]
+        w = [jnp.exp(s[h] - peak[h]) for h in each]
+        u = [jnp.exp(a[h] - peak[h]) for h in each]
+        weight = [jnp.sum(w[h], 1, keepdims=True) + jnp.sum(u[h], 1, keepdims=True) for h in each]
+        o = [
+            dot(w[h].astype(BF16), v[h], ((1,), (0,))) + dot(u[h].astype(BF16), av[h], ((1,), (0,)))
+            for h in each
+        ]
+        for h in each:
+            os_[pl.ds(base + h, block, stride=group), :] = o[h] / weight[h]
     ob[...] = os_[...].reshape(block, group, width).astype(BF16)
     save = pltpu.make_async_copy(ob, out.at[:, heads, :], sems.at[5])
     save.start()

time: 119 us -> 117 us (0.983)
  Pallas kernels: 34 us -> 30 us
  waiting for transfers between devices: 28.5 us -> 30.5 us
    pallas_call x4, Pallas kernels: 19.1 us -> 15.4 us  [block_part(): pl.pallas_call(functools.partial(block_kernel, first, tables, len(cands),...]
    ppermute x8, waiting for transfers between devices: 14.1 us -> 16.1 us  [body(): y_got.append(lax.ppermute(pay, 'hst', y_pairs[s]))]
  transfers between devices with their start and end apart: 17 -> 17, of which waited for: 10 -> 11; matrix products, arithmetic and copies ran while one was open for 1% -> 1% of each run, Pallas kernels for 23% -> 21%
where the time goes in v1:
time: 117 us; the launch traced here: 116 us
  starting transfers between devices  47 us (40%)
  waiting for transfers between devices  30.5 us (26%)
  Pallas kernels  30 us (26%)
  local copies, waits for them, and re-layouts  4.51 us (4%)
  other arithmetic  2.16 us (2%)
  between operations  1.69 us (1%)
    ppermute x8, starting transfers between devices, body(): y_got.append(lax.ppermute(pay, 'hst', y_pairs[s]))  17.4 us
    ppermute x7, starting transfers between devices, body(): z_new = lax.ppermute(pay, 'hst', z_pairs[s])  17 us
    ppermute x8, waiting for transfers between devices, body(): y_got.append(lax.ppermute(pay, 'hst', y_pairs[s]))  16.1 us
    pallas_call x4, Pallas kernels, block_part(): pl.pallas_call(functools.partial(block_kernel, first, tables, len(cands),...  15.4 us
    ppermute x7, waiting for transfers between devices, body(): z_new = lax.ppermute(pay, 'hst', z_pairs[s])  14.4 us
    all_to_all x1, starting transfers between devices, body(): back = lax.all_to_all(parts, 'hst', split_axis=0, concat_axis=0, tiled=True)  9.02 us
    pallas_call x1, Pallas kernels, part(): pl.pallas_call(functools.partial(part_kernel, rows, scale), grid=(groups,...  6.34 us
    unnamed x46, local copies, waits for them, and re-layouts  4.51 us
  transfers between devices with their start and end apart: 17, of which 11 were waited for; matrix products, arithmetic and copies ran while one was open for 1% of the time, Pallas kernels for 21%

profile of v1, /device:TPU:0, one launch (start us, length us, event | category | flops | bytes accessed | tf_op | source)
XLA Modules:
  0.0 115.9 jit_solution(4282922013418421202)
XLA Ops:
  0.6 1.9 %chunks.3 = (bf16[128,8,128]{2,1,0:T(8,128)(2,1)}, bf16[128,8,128]{2,1,0:T(8,128)(2,1)}) custom-call(bf16[192,32,128]{2,1,0:T(8,128)(2,1)} %key.13, bf16[192,32,128]{2,1,0:T(8,128)(2,1)} %value.13), custom_call_target="tpu_custom_call" | custom-call | tf_op jit(solution)/shard_map/chunks/pallas_call | solution.py:198
  2.5 3.9 %collective-permute-start.1 = (bf16[128,8,128]{2,1,0:T(8,128)(2,1)}, bf16[128,8,128]{2,1,0:T(8,128)(2,1)S(1)}, u32[]{:S(2)}, u32[]{:S(2)}) collective-permute-start(bf16[128,8,128]{2,1,0:T(8,128)(2,1)} %get-tuple-element.14), channel_id=1, source_target_pairs={{0,4},{1,5},{16,20},{17,21}} | collective-permute-start | bytes 786440 | tf_op jit(solution)/shard_map/ppermute | solution.py:377
  6.5 1.3 %collective-permute-start = (bf16[128,8,128]{2,1,0:T(8,128)(2,1)}, bf16[128,8,128]{2,1,0:T(8,128)(2,1)S(1)}, u32[]{:S(2)}, u32[]{:S(2)}) collective-permute-start(bf16[128,8,128]{2,1,0:T(8,128)(2,1)} %get-tuple-element.12), channel_id=1, source_target_pairs={{0,2},{1,3},{16,18},{17,19}} | collective-permute-start | bytes 786440 | tf_op jit(solution)/shard_map/ppermute | solution.py:385
  7.8 2.6 %chunks.2 = (bf16[128,8,128]{2,1,0:T(8,128)(2,1)}, bf16[128,8,128]{2,1,0:T(8,128)(2,1)}, bf16[128,8,128]{2,1,0:T(8,128)(2,1)}, bf16[128,8,128]{2,1,0:T(8,128)(2,...) custom-call(bf16[192,32,128]{2,1,0:T(8,128)(2,1)} %key.13, bf16[192,32,128]{2,1,0:T(8,128)(2,1)} %value.13), custom_call_target="tpu_custom_call" | custom-call | tf_op jit(solution)/shard_map/chunks/pallas_call | solution.py:198
  10.4 1.9 %collective-permute-done.1.rest_0_ = bf16[128,8,128]{2,1,0:T(8,128)(2,1)S(1)} collective-permute-done((bf16[128,8,128]{2,1,0:T(8,128)(2,1)}, bf16[128,8,128]{2,1,0:T(8,128)(2,1)S(1)}, u32[]{:S(2)}, u32[]{:S(2)}) %collective-permute-start.1) | collective-permute-done | bytes 262176 | tf_op jit(solution)/shard_map/ppermute | solution.py:377
  12.3 1.3 %collective-permute-done.rest_0_ = bf16[128,8,128]{2,1,0:T(8,128)(2,1)S(1)} collective-permute-done((bf16[128,8,128]{2,1,0:T(8,128)(2,1)}, bf16[128,8,128]{2,1,0:T(8,128)(2,1)S(1)}, u32[]{:S(2)}, u32[]{:S(2)}) %collective-permute-start) | collective-permute-done | bytes 262176 | tf_op jit(solution)/shard_map/ppermute | solution.py:385
  14.8 2.0 %collective-permute-start.2 = (bf16[128,8,128]{2,1,0:T(8,128)(2,1)S(1)}, bf16[128,8,128]{2,1,0:T(8,128)(2,1)S(1)}, u32[]{:S(2)}, u32[]{:S(2)}) collective-permute-start(bf16[128,8,128]{2,1,0:T(8,128)(2,1)S(1)} %get-tuple-element.25), channel_id=1, source_target_pairs={{0,4},{2,6},{4,8},{1,5},{3,7},{5,9},{16,20},{18,22},{20,24},{17,21... | collective-permute-start | bytes 786440 | tf_op jit(solution)/shard_map/ppermute | solution.py:377
  16.8 2.6 %collective-permute-start.4 = (bf16[128,8,128]{2,1,0:T(8,128)(2,1)S(1)}, bf16[128,8,128]{2,1,0:T(8,128)(2,1)S(1)}, u32[]{:S(2)}, u32[]{:S(2)}) collective-permute-start(bf16[128,8,128]{2,1,0:T(8,128)(2,1)S(1)} %get-tuple-element.24), channel_id=1, source_target_pairs={{0,2},{4,6},{1,3},{5,7},{16,18},{20,22},{17,19},{21,23}} | collective-permute-start | bytes 786440 | tf_op jit(solution)/shard_map/ppermute | solution.py:385
  19.4 2.1 %collective-permute-done.2.rest_1_.rest_6_ = bf16[128,8,128]{2,1,0:T(8,128)(2,1)S(1)} collective-permute-done((bf16[128,8,128]{2,1,0:T(8,128)(2,1)S(1)}, bf16[128,8,128]{2,1,0:T(8,128)(2,1)S(1)}, u32[]{:S(2)}, u32[]{:S(2)}) %collective-permute-start.2) | collective-permute-done | bytes 262176 | tf_op jit(solution)/shard_map/ppermute | solution.py:377
  21.5 2.6 %collective-permute-done.4.rest_2_.rest_7_ = bf16[128,8,128]{2,1,0:T(8,128)(2,1)S(1)} collective-permute-done((bf16[128,8,128]{2,1,0:T(8,128)(2,1)S(1)}, bf16[128,8,128]{2,1,0:T(8,128)(2,1)S(1)}, u32[]{:S(2)}, u32[]{:S(2)}) %collective-permute-start.4) | collective-permute-done | bytes 262176 | tf_op jit(solution)/shard_map/ppermute | solution.py:385
  24.2 4.4 %collective-permute-start.3 = (bf16[128,8,128]{2,1,0:T(8,128)(2,1)S(1)}, bf16[128,8,128]{2,1,0:T(8,128)(2,1)S(1)}, u32[]{:S(2)}, u32[]{:S(2)}) collective-permute-start(bf16[128,8,128]{2,1,0:T(8,128)(2,1)S(1)} %get-tuple-element.23), channel_id=1, source_target_pairs={{0,2},{4,6},{6,4},{8,10},{1,3},{5,7},{7,5},{9,11},{16,18},{20,22},... | collective-permute-start | bytes 786440 | tf_op jit(solution)/shard_map/ppermute | solution.py:385
  28.6 1.3 %collective-permute-start.5 = (bf16[128,8,128]{2,1,0:T(8,128)(2,1)S(1)}, bf16[128,8,128]{2,1,0:T(8,128)(2,1)S(1)}, u32[]{:S(2)}, u32[]{:S(2)}) collective-permute-start(bf16[128,8,128]{2,1,0:T(8,128)(2,1)S(1)} %get-tuple-element.22), channel_id=1, source_target_pairs={{0,4},{2,6},{4,8},{6,10},{8,12},{1,5},{3,7},{5,9},{7,11},{9,13},{1... | collective-permute-start | bytes 786440 | tf_op jit(solution)/shard_map/ppermute | solution.py:377
  29.9 2.5 %collective-permute-done.3.rest_4_.rest_8_.rest_3_.rest_6_ = bf16[128,8,128]{2,1,0:T(8,128)(2,1)S(1)} collective-permute-done((bf16[128,8,128]{2,1,0:T(8,128)(2,1)S(1)}, bf16[128,8,128]{2,1,0:T(8,128)(2,1)S(1)}, u32[]{:S(2)}, u32[]{:S(2)}) %collective-permute-start.3) | collective-permute-done | bytes 262176 | tf_op jit(solution)/shard_map/ppermute | solution.py:385
  32.5 1.3 %collective-permute-done.5.rest_3_.rest_7_.rest_2_.rest_8_.rest_0_ = bf16[128,8,128]{2,1,0:T(8,128)(2,1)S(1)} collective-permute-done((bf16[128,8,128]{2,1,0:T(8,128)(2,1)S(1)}, bf16[128,8,128]{2,1,0:T(8,128)(2,1)S(1)}, u32[]{:S(2)}, u32[]{:S(2)}) %collective-permute-start.5) | collective-permute-done | bytes 262176 | tf_op jit(solution)/shard_map/ppermute | solution.py:377
  33.9 4.5 %collective-permute-start.6 = (bf16[128,8,128]{2,1,0:T(8,128)(2,1)S(1)}, bf16[128,8,128]{2,1,0:T(8,128)(2,1)S(1)}, u32[]{:S(2)}, u32[]{:S(2)}) collective-permute-start(bf16[128,8,128]{2,1,0:T(8,128)(2,1)S(1)} %get-tuple-element.19), channel_id=1, source_target_pairs={{0,4},{2,6},{4,8},{6,10},{8,12},{10,14},{1,5},{3,7},{5,9},{7,11},{... | collective-permute-start | bytes 786440 | tf_op jit(solution)/shard_map/ppermute | solution.py:377
  39.1 1.7 %pack.1 = bf16[8,9,32,128]{3,2,1,0:T(8,128)(2,1)} custom-call(s32[1]{0:T(128)S(6)} %copy.14.valid, s32[8]{0:T(128)} %position.1, bf16[8,32,128]{2,1,0:T(8,128)(2,1)} %query.9), custom_call_target="tpu_custom_call" | custom-call | tf_op jit(solution)/shard_map/pack/pallas_call | solution.py:45
  40.8 3.5 %all-to-all-start = ((bf16[8,9,32,128]{3,2,1,0:T(8,128)(2,1)}), bf16[8,9,32,128]{3,2,1,0:T(8,128)(2,1)S(1)}, u32[]{:S(2)}, u32[]{:S(2)}) async-start(bf16[8,9,32,128]{3,2,1,0:T(8,128)(2,1)} %pack.1), calls=%async_computation | async-start | bytes 1179648 | tf_op jit(solution)/shard_map/all_to_all | solution.py:390
  44.5 3.8 %collective-permute-start.7 = (bf16[128,8,128]{2,1,0:T(8,128)(2,1)S(1)}, bf16[128,8,128]{2,1,0:T(8,128)(2,1)S(1)}, u32[]{:S(2)}, u32[]{:S(2)}) collective-permute-start(bf16[128,8,128]{2,1,0:T(8,128)(2,1)S(1)} %get-tuple-element.21), channel_id=1, source_target_pairs={{0,4},{4,8},{6,10},{8,12},{10,14},{1,5},{5,9},{7,11},{9,13},{11,15... | collective-permute-start | bytes 786440 | tf_op jit(solution)/shard_map/ppermute | solution.py:377
  48.3 9.1 %collective-permute-done.7.rest_11_.rest_3_.rest_7_.rest_0_.rest_8_ = bf16[128,8,128]{2,1,0:T(8,128)(2,1)S(1)} collective-permute-done((bf16[128,8,128]{2,1,0:T(8,128)(2,1)S(1)}, bf16[128,8,128]{2,1,0:T(8,128)(2,1)S(1)}, u32[]{:S(2)}, u32[]{:S(2)}) %collective-permute-start.7) | collective-permute-done | bytes 262176 | tf_op jit(solution)/shard_map/ppermute | solution.py:377
  58.9 6.3 %part.1 = bf16[8,35,8,128]{3,2,1,0:T(8,128)(2,1)} custom-call(s32[1]{0:T(128)S(6)} %copy.14.valid, bf16[8,9,32,128]{3,2,1,0:T(8,128)(2,1)} %copy-done.7, bf16[8,9,32,128]{3,2,1,0:T(8,128)(2,1)} %copy-done.7, bf16[192,32,128]{2,1,0:T(8,128)(2,1)} %key.13, bf16[192,32,128]{2,1,0:T(8,128)(2,1)} %value.13), custom_call_target="tpu_custom_call" | custom-call | tf_op jit(solution)/shard_map/part/pallas_call | solution.py:119
  65.3 9.0 %all-to-all-start.1 = ((bf16[8,35,8,128]{3,2,1,0:T(8,128)(2,1)}), bf16[8,35,8,128]{3,2,1,0:T(8,128)(2,1)S(1)}, u32[]{:S(2)}, u32[]{:S(2)}) async-start(bf16[8,35,8,128]{3,2,1,0:T(8,128)(2,1)} %part.1), calls=%async_computation.1 | async-start | bytes 1146880 | tf_op jit(solution)/shard_map/all_to_all | solution.py:392
  74.3 3.9 %collective-permute-start.14 = (bf16[128,8,128]{2,1,0:T(8,128)(2,1)S(1)}, bf16[128,8,128]{2,1,0:T(8,128)(2,1)S(1)}, u32[]{:S(2)}, u32[]{:S(2)}) collective-permute-start(bf16[128,8,128]{2,1,0:T(8,128)(2,1)S(1)} %get-tuple-element.18), channel_id=1, source_target_pairs={{0,2},{4,6},{6,4},{8,10},{10,8},{12,14},{1,3},{5,7},{7,5},{9,11},{... | collective-permute-start | bytes 786440 | tf_op jit(solution)/shard_map/ppermute | solution.py:385
  78.2 1.3 %collective-permute-start.13 = (bf16[128,8,128]{2,1,0:T(8,128)(2,1)S(1)}, bf16[128,8,128]{2,1,0:T(8,128)(2,1)S(1)}, u32[]{:S(2)}, u32[]{:S(2)}) collective-permute-start(bf16[128,8,128]{2,1,0:T(8,128)(2,1)S(1)} %get-tuple-element.20), channel_id=1, source_target_pairs={{0,2},{4,6},{6,4},{8,10},{10,8},{12,14},{14,12},{1,3},{5,7},{7,5},... | collective-permute-start | bytes 786440 | tf_op jit(solution)/shard_map/ppermute | solution.py:385
  81.0 1.3 %collective-permute-start.9 = (bf16[128,8,128]{2,1,0:T(8,128)(2,1)}, bf16[128,8,128]{2,1,0:T(8,128)(2,1)S(1)}, u32[]{:S(2)}, u32[]{:S(2)}) collective-permute-start(bf16[128,8,128]{2,1,0:T(8,128)(2,1)} %broadcast_select_fusion.4), channel_id=1, source_target_pairs={{0,2},{4,6},{8,10},{10,8},{12,14},{14,12},{1,3},{5,7},{9,11},{11,9... | collective-permute-start | bytes 786440 | tf_op jit(solution)/shard_map/ppermute | solution.py:385
  82.3 1.3 %collective-permute-start.11 = (bf16[128,8,128]{2,1,0:T(8,128)(2,1)S(1)}, bf16[128,8,128]{2,1,0:T(8,128)(2,1)S(1)}, u32[]{:S(2)}, u32[]{:S(2)}) collective-permute-start(bf16[128,8,128]{2,1,0:T(8,128)(2,1)S(1)} %broadcast_select_fusion.3), channel_id=1, source_target_pairs={{0,2},{8,10},{12,14},{14,12},{1,3},{9,11},{13,15},{15,13},{16,18},... | collective-permute-start | bytes 786440 | tf_op jit(solution)/shard_map/ppermute | solution.py:385
  83.7 1.3 %collective-permute-start.12 = (bf16[128,8,128]{2,1,0:T(8,128)(2,1)S(1)}, bf16[128,8,128]{2,1,0:T(8,128)(2,1)S(1)}, u32[]{:S(2)}, u32[]{:S(2)}) collective-permute-start(bf16[128,8,128]{2,1,0:T(8,128)(2,1)S(1)} %broadcast_select_fusion.2), channel_id=1, source_target_pairs={{0,2},{12,14},{1,3},{13,15},{16,18},{28,30},{17,19},{29,31}} | collective-permute-start | bytes 786440 | tf_op jit(solution)/shard_map/ppermute | solution.py:385
  86.1 6.5 %collective-permute-done.13.rest_11_.rest_6_.rest_12_.rest_4_.rest_8_.rest_9_ = bf16[128,8,128]{2,1,0:T(8,128)(2,1)S(1)} collective-permute-done((bf16[128,8,128]{2,1,0:T(8,128)(2,1)S(1)}, bf16[128,8,128]{2,1,0:T(8,128)(2,1)S(1)}, u32[]{:S(2)}, u32[]{:S(2)}) %collective-permute-start.13) | collective-permute-done | bytes 262176 | tf_op jit(solution)/shard_map/ppermute | solution.py:385
  93.3 3.8 %shard_map.77.rest_14_ = bf16[192,32,128]{2,1,0:T(8,128)(2,1)} custom-call(s32[1]{0:T(128)S(6)} %copy.14.valid, bf16[192,32,128]{2,1,0:T(8,128)(2,1)} %query.8, bf16[192,32,128]{2,1,0:T(8,128)(2,1)} %key.13, bf16[192,32,128]{2,1,0:T(8,128)(2,1)} %value.13, bf16[128,8,128]{2,1,0:T(8,128)(2,1)} %copy-done.14, bf16[128,8,128]{2,1,0:T(8,128)(2,1)} %copy-done.8, ...), custom_call_target="tpu_custom_call" | custom-call | tf_op jit(solution)/shard_map/pallas_call | solution.py:289
  99.0 3.9 %shard_map.78.rest_12_ = bf16[192,32,128]{2,1,0:T(8,128)(2,1)} custom-call(s32[1]{0:T(128)S(6)} %copy.14.valid, bf16[192,32,128]{2,1,0:T(8,128)(2,1)} %query.8, bf16[192,32,128]{2,1,0:T(8,128)(2,1)} %key.13, bf16[192,32,128]{2,1,0:T(8,128)(2,1)} %value.13, bf16[128,8,128]{2,1,0:T(8,128)(2,1)} %copy-done.13, ...), custom_call_target="tpu_custom_call", output_to_operand_aliasing={{}: (18, {})} | custom-call | tf_op jit(solution)/shard_map/pallas_call | solution.py:289
  104.6 3.8 %shard_map.79.rest_13_ = bf16[192,32,128]{2,1,0:T(8,128)(2,1)} custom-call(s32[1]{0:T(128)S(6)} %copy.14.valid, bf16[192,32,128]{2,1,0:T(8,128)(2,1)} %query.8, bf16[192,32,128]{2,1,0:T(8,128)(2,1)} %key.13, bf16[192,32,128]{2,1,0:T(8,128)(2,1)} %value.13, bf16[128,8,128]{2,1,0:T(8,128)(2,1)} %copy-done.2, ...), custom_call_target="tpu_custom_call", output_to_operand_aliasing={{}: (16, {})} | custom-call | tf_op jit(solution)/shard_map/pallas_call | solution.py:289
  109.2 2.1 %merge.1 = bf16[8,32,128]{2,1,0:T(8,128)(2,1)} custom-call(bf16[8,35,8,128]{3,2,1,0:T(8,128)(2,1)} %copy-done.12), custom_call_target="tpu_custom_call" | custom-call | tf_op jit(solution)/shard_map/merge/pallas_call | solution.py:164
  112.1 3.8 %shard_map.80 = bf16[192,32,128]{2,1,0:T(8,128)(2,1)} custom-call(s32[1]{0:T(128)S(6)} %copy.14.valid, bf16[192,32,128]{2,1,0:T(8,128)(2,1)} %query.8, bf16[192,32,128]{2,1,0:T(8,128)(2,1)} %key.13, bf16[192,32,128]{2,1,0:T(8,128)(2,1)} %value.13, bf16[128,8,128]{2,1,0:T(8,128)(2,1)} %copy-done.3, ...), custom_call_target="tpu_custom_call", output_to_operand_aliasing={{}: (17, {})} | custom-call | tf_op jit(solution)/shard_map/pallas_call | solution.py:289
  (64 shorter events, 11.2 us)
Async XLA Ops:
  2.5 9.8 %collective-permute-start.1 = (bf16[128,8,128]{2,1,0:T(8,128)(2,1)}, bf16[128,8,128]{2,1,0:T(8,128)(2,1)S(1)}, u32[]{:S(2)}, u32[]{:S(2)}) collective-permute-start(bf16[128,8,128]{2,1,0:T(8,128)(2,1)} %get-tuple-element.14), channel_id=1, source_target_pairs={{0,4},{1,5},{16,20},{17,21}} | collective-permute-start | bytes 786440 | tf_op jit(solution)/shard_map/ppermute | solution.py:377
  6.5 7.2 %collective-permute-start = (bf16[128,8,128]{2,1,0:T(8,128)(2,1)}, bf16[128,8,128]{2,1,0:T(8,128)(2,1)S(1)}, u32[]{:S(2)}, u32[]{:S(2)}) collective-permute-start(bf16[128,8,128]{2,1,0:T(8,128)(2,1)} %get-tuple-element.12), channel_id=1, source_target_pairs={{0,2},{1,3},{16,18},{17,19}} | collective-permute-start | bytes 786440 | tf_op jit(solution)/shard_map/ppermute | solution.py:385
  10.4 13.7 %copy-start.19 = (bf16[128,8,128]{2,1,0:T(8,128)(2,1)S(1)}, bf16[128,8,128]{2,1,0:T(8,128)(2,1)}, u32[]{:S(2)}) copy-start(bf16[128,8,128]{2,1,0:T(8,128)(2,1)} %get-tuple-element.17) | copy-start | bytes 786436
  10.4 13.7 %copy-start.22 = (bf16[128,8,128]{2,1,0:T(8,128)(2,1)S(1)}, bf16[128,8,128]{2,1,0:T(8,128)(2,1)}, u32[]{:S(2)}) copy-start(bf16[128,8,128]{2,1,0:T(8,128)(2,1)} %get-tuple-element.11) | copy-start | bytes 786436
  12.3 11.9 %copy-start.14 = (bf16[128,8,128]{2,1,0:T(8,128)(2,1)}, bf16[128,8,128]{2,1,0:T(8,128)(2,1)S(1)}, u32[]{:S(2)}) copy-start(bf16[128,8,128]{2,1,0:T(8,128)(2,1)S(1)} %collective-permute-done.1.rest_0_) | copy-start | bytes 786436
  13.6 10.6 %copy-start.13 = (bf16[128,8,128]{2,1,0:T(8,128)(2,1)}, bf16[128,8,128]{2,1,0:T(8,128)(2,1)S(1)}, u32[]{:S(2)}) copy-start(bf16[128,8,128]{2,1,0:T(8,128)(2,1)S(1)} %collective-permute-done.rest_0_) | copy-start | bytes 786436
  13.6 20.2 %copy-start.18 = (bf16[128,8,128]{2,1,0:T(8,128)(2,1)S(1)}, bf16[128,8,128]{2,1,0:T(8,128)(2,1)}, u32[]{:S(2)}) copy-start(bf16[128,8,128]{2,1,0:T(8,128)(2,1)} %get-tuple-element.15) | copy-start | bytes 786436
  13.6 20.2 %copy-start.21 = (bf16[128,8,128]{2,1,0:T(8,128)(2,1)S(1)}, bf16[128,8,128]{2,1,0:T(8,128)(2,1)}, u32[]{:S(2)}) copy-start(bf16[128,8,128]{2,1,0:T(8,128)(2,1)} %get-tuple-element.14) | copy-start | bytes 786436
  14.8 6.7 %collective-permute-start.2 = (bf16[128,8,128]{2,1,0:T(8,128)(2,1)S(1)}, bf16[128,8,128]{2,1,0:T(8,128)(2,1)S(1)}, u32[]{:S(2)}, u32[]{:S(2)}) collective-permute-start(bf16[128,8,128]{2,1,0:T(8,128)(2,1)S(1)} %get-tuple-element.25), channel_id=1, source_target_pairs={{0,4},{2,6},{4,8},{1,5},{3,7},{5,9},{16,20},{18,22},{20,24},{17,21... | collective-permute-start | bytes 786440 | tf_op jit(solution)/shard_map/ppermute | solution.py:377
  16.8 7.3 %collective-permute-start.4 = (bf16[128,8,128]{2,1,0:T(8,128)(2,1)S(1)}, bf16[128,8,128]{2,1,0:T(8,128)(2,1)S(1)}, u32[]{:S(2)}, u32[]{:S(2)}) collective-permute-start(bf16[128,8,128]{2,1,0:T(8,128)(2,1)S(1)} %get-tuple-element.24), channel_id=1, source_target_pairs={{0,2},{4,6},{1,3},{5,7},{16,18},{20,22},{17,19},{21,23}} | collective-permute-start | bytes 786440 | tf_op jit(solution)/shard_map/ppermute | solution.py:385
  21.5 12.4 %copy-start.8 = (bf16[128,8,128]{2,1,0:T(8,128)(2,1)}, bf16[128,8,128]{2,1,0:T(8,128)(2,1)S(1)}, u32[]{:S(2)}) copy-start(bf16[128,8,128]{2,1,0:T(8,128)(2,1)S(1)} %collective-permute-done.2.rest_1_.rest_6_) | copy-start | bytes 786436
  24.1 9.8 %copy-start.11 = (bf16[128,8,128]{2,1,0:T(8,128)(2,1)}, bf16[128,8,128]{2,1,0:T(8,128)(2,1)S(1)}, u32[]{:S(2)}) copy-start(bf16[128,8,128]{2,1,0:T(8,128)(2,1)S(1)} %collective-permute-done.4.rest_2_.rest_7_) | copy-start | bytes 786436
  24.2 8.3 %collective-permute-start.3 = (bf16[128,8,128]{2,1,0:T(8,128)(2,1)S(1)}, bf16[128,8,128]{2,1,0:T(8,128)(2,1)S(1)}, u32[]{:S(2)}, u32[]{:S(2)}) collective-permute-start(bf16[128,8,128]{2,1,0:T(8,128)(2,1)S(1)} %get-tuple-element.23), channel_id=1, source_target_pairs={{0,2},{4,6},{6,4},{8,10},{1,3},{5,7},{7,5},{9,11},{16,18},{20,22},... | collective-permute-start | bytes 786440 | tf_op jit(solution)/shard_map/ppermute | solution.py:385
  28.6 5.2 %collective-permute-start.5 = (bf16[128,8,128]{2,1,0:T(8,128)(2,1)S(1)}, bf16[128,8,128]{2,1,0:T(8,128)(2,1)S(1)}, u32[]{:S(2)}, u32[]{:S(2)}) collective-permute-start(bf16[128,8,128]{2,1,0:T(8,128)(2,1)S(1)} %get-tuple-element.22), channel_id=1, source_target_pairs={{0,4},{2,6},{4,8},{6,10},{8,12},{1,5},{3,7},{5,9},{7,11},{9,13},{1... | collective-permute-start | bytes 786440 | tf_op jit(solution)/shard_map/ppermute | solution.py:377
  32.5 8.4 %copy-start.6 = (bf16[128,8,128]{2,1,0:T(8,128)(2,1)}, bf16[128,8,128]{2,1,0:T(8,128)(2,1)S(1)}, u32[]{:S(2)}) copy-start(bf16[128,8,128]{2,1,0:T(8,128)(2,1)S(1)} %collective-permute-done.3.rest_4_.rest_8_.rest_3_.rest_6_) | copy-start | bytes 786436
  33.8 10.6 %copy-start.15 = (bf16[128,8,128]{2,1,0:T(8,128)(2,1)S(1)}, bf16[128,8,128]{2,1,0:T(8,128)(2,1)}, u32[]{:S(2)}) copy-start(bf16[128,8,128]{2,1,0:T(8,128)(2,1)} %get-tuple-element.10) | copy-start | bytes 786436
  33.8 10.6 %copy-start.16 = (bf16[128,8,128]{2,1,0:T(8,128)(2,1)S(1)}, bf16[128,8,128]{2,1,0:T(8,128)(2,1)}, u32[]{:S(2)}) copy-start(bf16[128,8,128]{2,1,0:T(8,128)(2,1)} %get-tuple-element.13) | copy-start | bytes 786436
  33.9 10.5 %collective-permute-start.6 = (bf16[128,8,128]{2,1,0:T(8,128)(2,1)S(1)}, bf16[128,8,128]{2,1,0:T(8,128)(2,1)S(1)}, u32[]{:S(2)}, u32[]{:S(2)}) collective-permute-start(bf16[128,8,128]{2,1,0:T(8,128)(2,1)S(1)} %get-tuple-element.19), channel_id=1, source_target_pairs={{0,4},{2,6},{4,8},{6,10},{8,12},{10,14},{1,5},{3,7},{5,9},{7,11},{... | collective-permute-start | bytes 786440 | tf_op jit(solution)/shard_map/ppermute | solution.py:377
  40.8 17.3 %all-to-all-start = ((bf16[8,9,32,128]{3,2,1,0:T(8,128)(2,1)}), bf16[8,9,32,128]{3,2,1,0:T(8,128)(2,1)S(1)}, u32[]{:S(2)}, u32[]{:S(2)}) async-start(bf16[8,9,32,128]{3,2,1,0:T(8,128)(2,1)} %pack.1), calls=%async_computation | async-start | bytes 1179648 | tf_op jit(solution)/shard_map/all_to_all | solution.py:390
  44.4 20.9 %copy-start = (bf16[128,8,128]{2,1,0:T(8,128)(2,1)}, bf16[128,8,128]{2,1,0:T(8,128)(2,1)S(1)}, u32[]{:S(2)}) copy-start(bf16[128,8,128]{2,1,0:T(8,128)(2,1)S(1)} %collective-permute-done.6.rest_9_.rest_4_.rest_1_.rest_6_.rest_7_) | copy-start | bytes 786436
  44.5 13.0 %collective-permute-start.7 = (bf16[128,8,128]{2,1,0:T(8,128)(2,1)S(1)}, bf16[128,8,128]{2,1,0:T(8,128)(2,1)S(1)}, u32[]{:S(2)}, u32[]{:S(2)}) collective-permute-start(bf16[128,8,128]{2,1,0:T(8,128)(2,1)S(1)} %get-tuple-element.21), channel_id=1, source_target_pairs={{0,4},{4,8},{6,10},{8,12},{10,14},{1,5},{5,9},{7,11},{9,13},{11,15... | collective-permute-start | bytes 786440 | tf_op jit(solution)/shard_map/ppermute | solution.py:377
  57.4 22.8 %copy-start.3 = (bf16[128,8,128]{2,1,0:T(8,128)(2,1)}, bf16[128,8,128]{2,1,0:T(8,128)(2,1)S(1)}, u32[]{:S(2)}) copy-start(bf16[128,8,128]{2,1,0:T(8,128)(2,1)S(1)} %collective-permute-done.7.rest_11_.rest_3_.rest_7_.rest_0_.rest_8_) | copy-start | bytes 786436
  57.4 22.1 %collective-permute-start.8 = (bf16[128,8,128]{2,1,0:T(8,128)(2,1)S(1)}, bf16[128,8,128]{2,1,0:T(8,128)(2,1)S(1)}, u32[]{:S(2)}, u32[]{:S(2)}) collective-permute-start(bf16[128,8,128]{2,1,0:T(8,128)(2,1)S(1)} %collective-permute-done.7.rest_11_.rest_3_.rest_7_.rest_0_.rest_8_), channel_id=1, source_target_pairs={{4,8},{8,12},{10,14},{5,9},{9,13},{11,15},{20,24},{24,28},{26,30},... | collective-permute-start | bytes 786440 | tf_op jit(solution)/shard_map/ppermute | solution.py:377
  65.3 43.1 %all-to-all-start.1 = ((bf16[8,35,8,128]{3,2,1,0:T(8,128)(2,1)}), bf16[8,35,8,128]{3,2,1,0:T(8,128)(2,1)S(1)}, u32[]{:S(2)}, u32[]{:S(2)}) async-start(bf16[8,35,8,128]{3,2,1,0:T(8,128)(2,1)} %part.1), calls=%async_computation.1 | async-start | bytes 1146880 | tf_op jit(solution)/shard_map/all_to_all | solution.py:392
  74.3 11.8 %collective-permute-start.14 = (bf16[128,8,128]{2,1,0:T(8,128)(2,1)S(1)}, bf16[128,8,128]{2,1,0:T(8,128)(2,1)S(1)}, u32[]{:S(2)}, u32[]{:S(2)}) collective-permute-start(bf16[128,8,128]{2,1,0:T(8,128)(2,1)S(1)} %get-tuple-element.18), channel_id=1, source_target_pairs={{0,2},{4,6},{6,4},{8,10},{10,8},{12,14},{1,3},{5,7},{7,5},{9,11},{... | collective-permute-start | bytes 786440 | tf_op jit(solution)/shard_map/ppermute | solution.py:385
  78.2 14.4 %collective-permute-start.13 = (bf16[128,8,128]{2,1,0:T(8,128)(2,1)S(1)}, bf16[128,8,128]{2,1,0:T(8,128)(2,1)S(1)}, u32[]{:S(2)}, u32[]{:S(2)}) collective-permute-start(bf16[128,8,128]{2,1,0:T(8,128)(2,1)S(1)} %get-tuple-element.20), channel_id=1, source_target_pairs={{0,2},{4,6},{6,4},{8,10},{10,8},{12,14},{14,12},{1,3},{5,7},{7,5},... | collective-permute-start | bytes 786440 | tf_op jit(solution)/shard_map/ppermute | solution.py:385
  79.6 17.6 %copy-start.9 = (bf16[128,8,128]{2,1,0:T(8,128)(2,1)}, bf16[128,8,128]{2,1,0:T(8,128)(2,1)S(1)}, u32[]{:S(2)}) copy-start(bf16[128,8,128]{2,1,0:T(8,128)(2,1)S(1)} %collective-permute-done.8.rest_9_.rest_1_.rest_10_) | copy-start | bytes 786436
  79.6 4.1 %collective-permute-start.10 = (bf16[128,8,128]{2,1,0:T(8,128)(2,1)S(1)}, bf16[128,8,128]{2,1,0:T(8,128)(2,1)S(1)}, u32[]{:S(2)}, u32[]{:S(2)}) collective-permute-start(bf16[128,8,128]{2,1,0:T(8,128)(2,1)S(1)} %collective-permute-done.8.rest_9_.rest_1_.rest_10_), channel_id=1, source_target_pairs={{8,12},{9,13},{24,28},{25,29}} | collective-permute-start | bytes 786440 | tf_op jit(solution)/shard_map/ppermute | solution.py:377
  81.0 17.3 %collective-permute-start.9 = (bf16[128,8,128]{2,1,0:T(8,128)(2,1)}, bf16[128,8,128]{2,1,0:T(8,128)(2,1)S(1)}, u32[]{:S(2)}, u32[]{:S(2)}) collective-permute-start(bf16[128,8,128]{2,1,0:T(8,128)(2,1)} %broadcast_select_fusion.4), channel_id=1, source_target_pairs={{0,2},{4,6},{8,10},{10,8},{12,14},{14,12},{1,3},{5,7},{9,11},{11,9... | collective-permute-start | bytes 786440 | tf_op jit(solution)/shard_map/ppermute | solution.py:385
  82.3 21.5 %collective-permute-start.11 = (bf16[128,8,128]{2,1,0:T(8,128)(2,1)S(1)}, bf16[128,8,128]{2,1,0:T(8,128)(2,1)S(1)}, u32[]{:S(2)}, u32[]{:S(2)}) collective-permute-start(bf16[128,8,128]{2,1,0:T(8,128)(2,1)S(1)} %broadcast_select_fusion.3), channel_id=1, source_target_pairs={{0,2},{8,10},{12,14},{14,12},{1,3},{9,11},{13,15},{15,13},{16,18},... | collective-permute-start | bytes 786440 | tf_op jit(solution)/shard_map/ppermute | solution.py:385
  83.7 13.5 %copy-start.17 = (bf16[128,8,128]{2,1,0:T(8,128)(2,1)}, bf16[128,8,128]{2,1,0:T(8,128)(2,1)S(1)}, u32[]{:S(2)}) copy-start(bf16[128,8,128]{2,1,0:T(8,128)(2,1)S(1)} %collective-permute-done.10.rest_3_) | copy-start | bytes 786436
  83.7 27.7 %collective-permute-start.12 = (bf16[128,8,128]{2,1,0:T(8,128)(2,1)S(1)}, bf16[128,8,128]{2,1,0:T(8,128)(2,1)S(1)}, u32[]{:S(2)}, u32[]{:S(2)}) collective-permute-start(bf16[128,8,128]{2,1,0:T(8,128)(2,1)S(1)} %broadcast_select_fusion.2), channel_id=1, source_target_pairs={{0,2},{12,14},{1,3},{13,15},{16,18},{28,30},{17,19},{29,31}} | collective-permute-start | bytes 786440 | tf_op jit(solution)/shard_map/ppermute | solution.py:385
  (8 other events, 18.0 us)
